TPU v7x, 32 devices: a whole 2x2x4 slice. The times are simulated.
32 devices in a mesh: fsdp: 4 (over x, core), ctx: 8 (over z, y).
Axes of the slice: x: 2, y: 2, z: 4, core: 2. Of those that a mesh axis runs over, the one named last changes fastest.
Arguments:
- inputs: bfloat16 [8, 1024, 1600], P('fsdp', 'ctx'), may hold values from -6 to 6
- cotangent: bfloat16 [8, 1024, 1600], P('fsdp', 'ctx'), may hold values from -6 to 6
- segments: int32 [8, 1024], P('fsdp', 'ctx'), may hold values from 0 to 10, as said below
- stretch_order: int32 [8], replicated, may hold values from 0 to 7, as said below
- prenorm_gain: bfloat16 [1600], P('ctx'), may hold values from 0.5 to 1.5
- prenorm_shift: bfloat16 [1600], P('ctx'), may hold values from -2 to 2
- joint_weight: bfloat16 [1600, 4800], P('fsdp', 'ctx')
- query_bias: bfloat16 [1600], P('ctx'), may hold values from -2 to 2
- value_bias: bfloat16 [1600], P('ctx'), may hold values from -2 to 2
- mixer_weight: bfloat16 [1600, 1600], P('fsdp', 'ctx'), may hold values from -0.75 to 0.75
- mixer_bias: bfloat16 [1600], P('ctx'), may hold values from -2 to 2
- midnorm_gain: bfloat16 [1600], P('ctx'), may hold values from 0.5 to 1.5
- midnorm_shift: bfloat16 [1600], P('ctx'), may hold values from -2 to 2
- expand_weight: bfloat16 [1600, 6400], P('fsdp', 'ctx'), may hold values from -0.15625 to 0.15625
- expand_bias: bfloat16 [6400], P('ctx'), may hold values from -2 to 2
- shrink_weight: bfloat16 [6400, 1600], P('fsdp', 'ctx'), may hold values from -0.078125 to 0.078125
- shrink_bias: bfloat16 [1600], P('ctx'), may hold values from -2 to 2
Outputs:
- block_output: bfloat16 [8, 1024, 1600], P('fsdp', 'ctx')
- input_gradient: float32 [8, 1024, 1600], P('fsdp', 'ctx')
- prenormgain_gradient: float32 [1600], P('ctx')
- prenormshift_gradient: float32 [1600], P('ctx')
- joint_gradient: float32 [1600, 4800], P('fsdp', 'ctx')
- querybias_gradient: float32 [1600], P('ctx')
- valuebias_gradient: float32 [1600], P('ctx')
- mixer_gradient: float32 [1600, 1600], P('fsdp', 'ctx')
- mixerbias_gradient: float32 [1600], P('ctx')
- midnormgain_gradient: float32 [1600], P('ctx')
- midnormshift_gradient: float32 [1600], P('ctx')
- expand_gradient: float32 [1600, 6400], P('fsdp', 'ctx')
- expandbias_gradient: float32 [6400], P('ctx')
- shrink_gradient: float32 [6400, 1600], P('fsdp', 'ctx')
- shrinkbias_gradient: float32 [1600], P('ctx')
Inputs may be any that keep to these rules, and one draw needn't show every extreme that they name: A permutation: stored block i of every sequence is its true block stretch_order[i]. `segments`: in true order the numbers start at 0 and rise by one where a document starts; each document but a sequence's last spans 100 to 1000 positions.
All inputs are finite; a program needn't handle non-finite values.
Results may differ from a plain program's by a relative error of at most 0.019.
Values may be sent and summed in bfloat16 or wider, within the bound.
A program may use at most 320 MiB of HBM per device.

v0:
```python
import functools

import jax
import jax.numpy as jnp
from jax import lax
from jax.experimental import pallas as pl
from jax.experimental.pallas import tpu as pltpu
from jax.sharding import PartitionSpec as P


HEAD = 64
MICRO = 2
LANES = 128
STRETCH = 128
TILE = 256


epsilon = 1e-05
masked_score = -1e30


def layer_norm(values, gain, shift):
    center = values - jnp.mean(values, axis=-1, keepdims=True)
    spread = jnp.mean(center * center, axis=-1, keepdims=True)
    return center * lax.rsqrt(spread + epsilon) * gain + shift


def piece_size(count):
    size_now = min(count, 512)
    while count % size_now:
        size_now -= 1
    return size_now


def true_positions(stretch_order, first_index, count, stretch_len):
    stored = first_index + jnp.arange(count, dtype=jnp.int32)
    holder = stored // stretch_len
    picked = holder[:, None] == jnp.arange(stretch_order.shape[0], dtype=jnp.int32)[None, :]
    return (
        jnp.sum(jnp.where(picked, stretch_order[None, :], 0), axis=1) * stretch_len
        + stored % stretch_len
    )


def times_transposed(left, right):
    return lax.dot_general(
        left, right, (((1,), (1,)), ((), ())), preferred_element_type=jnp.float32
    )


def outer_sum(left, right):
    return lax.dot_general(
        left, right, (((0,), (0,)), ((), ())), preferred_element_type=jnp.float32
    )


def fetch_weights(local_parts):
    (
        joint_weight,
        mixer_weight,
        expand_weight,
        shrink_weight,
        prenorm_gain,
        prenorm_shift,
        query_bias,
        value_bias,
        mixer_bias,
        midnorm_gain,
        midnorm_shift,
        expand_bias,
        shrink_bias,
    ) = local_parts
    spread_out = (
        lax.all_gather(joint_weight, "ctx", axis=1, tiled=True),
        lax.all_gather(mixer_weight, "ctx", axis=1, tiled=True),
        lax.all_gather(expand_weight, "ctx", axis=1, tiled=True),
        lax.all_gather(shrink_weight, "ctx", axis=1, tiled=True),
        lax.all_gather(prenorm_gain, "ctx", axis=0, tiled=True),
        lax.all_gather(prenorm_shift, "ctx", axis=0, tiled=True),
        lax.all_gather(query_bias, "ctx", axis=0, tiled=True),
        lax.all_gather(value_bias, "ctx", axis=0, tiled=True),
        lax.all_gather(mixer_bias, "ctx", axis=0, tiled=True),
        lax.all_gather(midnorm_gain, "ctx", axis=0, tiled=True),
        lax.all_gather(midnorm_shift, "ctx", axis=0, tiled=True),
        lax.all_gather(expand_bias, "ctx", axis=0, tiled=True),
        lax.all_gather(shrink_bias, "ctx", axis=0, tiled=True),
    )
    whole_rows = (
        lax.all_gather(spread_out[0], "fsdp", axis=0, tiled=True),
        lax.all_gather(spread_out[1], "fsdp", axis=0, tiled=True),
        lax.all_gather(spread_out[2], "fsdp", axis=0, tiled=True),
        lax.all_gather(spread_out[3], "fsdp", axis=0, tiled=True),
    )
    return tuple(whole_rows) + tuple(spread_out[4:])


def reduce_gradients(matrices, smalls):
    small_sums = (
        lax.psum(smalls[0].astype(jnp.bfloat16), "fsdp").astype(jnp.float32),
        lax.psum(smalls[1].astype(jnp.bfloat16), "fsdp").astype(jnp.float32),
        lax.psum(smalls[2].astype(jnp.bfloat16), "fsdp").astype(jnp.float32),
        lax.psum(smalls[3].astype(jnp.bfloat16), "fsdp").astype(jnp.float32),
        lax.psum(smalls[4].astype(jnp.bfloat16), "fsdp").astype(jnp.float32),
        lax.psum(smalls[5].astype(jnp.bfloat16), "fsdp").astype(jnp.float32),
        lax.psum(smalls[6].astype(jnp.bfloat16), "fsdp").astype(jnp.float32),
        lax.psum(smalls[7].astype(jnp.bfloat16), "fsdp").astype(jnp.float32),
        lax.psum(smalls[8].astype(jnp.bfloat16), "fsdp").astype(jnp.float32),
    )
    column_part = (
        lax.psum_scatter(
            matrices[0].astype(jnp.bfloat16), "ctx", scatter_dimension=1, tiled=True
        ).astype(jnp.float32),
        lax.psum_scatter(
            matrices[1].astype(jnp.bfloat16), "ctx", scatter_dimension=1, tiled=True
        ).astype(jnp.float32),
        lax.psum_scatter(
            matrices[2].astype(jnp.bfloat16), "ctx", scatter_dimension=1, tiled=True
        ).astype(jnp.float32),
        lax.psum_scatter(
            matrices[3].astype(jnp.bfloat16), "ctx", scatter_dimension=1, tiled=True
        ).astype(jnp.float32),
        lax.psum_scatter(
            small_sums[0].astype(jnp.bfloat16), "ctx", scatter_dimension=0, tiled=True
        ).astype(jnp.float32),
        lax.psum_scatter(
            small_sums[1].astype(jnp.bfloat16), "ctx", scatter_dimension=0, tiled=True
        ).astype(jnp.float32),
        lax.psum_scatter(
            small_sums[2].astype(jnp.bfloat16), "ctx", scatter_dimension=0, tiled=True
        ).astype(jnp.float32),
        lax.psum_scatter(
            small_sums[3].astype(jnp.bfloat16), "ctx", scatter_dimension=0, tiled=True
        ).astype(jnp.float32),
        lax.psum_scatter(
            small_sums[4].astype(jnp.bfloat16), "ctx", scatter_dimension=0, tiled=True
        ).astype(jnp.float32),
        lax.psum_scatter(
            small_sums[5].astype(jnp.bfloat16), "ctx", scatter_dimension=0, tiled=True
        ).astype(jnp.float32),
        lax.psum_scatter(
            small_sums[6].astype(jnp.bfloat16), "ctx", scatter_dimension=0, tiled=True
        ).astype(jnp.float32),
        lax.psum_scatter(
            small_sums[7].astype(jnp.bfloat16), "ctx", scatter_dimension=0, tiled=True
        ).astype(jnp.float32),
        lax.psum_scatter(
            small_sums[8].astype(jnp.bfloat16), "ctx", scatter_dimension=0, tiled=True
        ).astype(jnp.float32),
    )
    row_part = (
        lax.psum_scatter(
            column_part[0].astype(jnp.bfloat16), "fsdp", scatter_dimension=0, tiled=True
        ).astype(jnp.float32),
        lax.psum_scatter(
            column_part[1].astype(jnp.bfloat16), "fsdp", scatter_dimension=0, tiled=True
        ).astype(jnp.float32),
        lax.psum_scatter(
            column_part[2].astype(jnp.bfloat16), "fsdp", scatter_dimension=0, tiled=True
        ).astype(jnp.float32),
        lax.psum_scatter(
            column_part[3].astype(jnp.bfloat16), "fsdp", scatter_dimension=0, tiled=True
        ).astype(jnp.float32),
    )
    return tuple(row_part) + tuple(column_part[4:])


def local(
    inputs,
    cotangent,
    segments,
    stretch_order,
    prenorm_gain,
    prenorm_shift,
    joint_weight,
    query_bias,
    value_bias,
    mixer_weight,
    mixer_bias,
    midnorm_gain,
    midnorm_shift,
    expand_weight,
    expand_bias,
    shrink_weight,
    shrink_bias,
):
    local_parts = (
        joint_weight,
        mixer_weight,
        expand_weight,
        shrink_weight,
        prenorm_gain,
        prenorm_shift,
        query_bias,
        value_bias,
        mixer_bias,
        midnorm_gain,
        midnorm_shift,
        expand_bias,
        shrink_bias,
    )
    seq_local, stretch_len, model_width = inputs.shape
    head_count = model_width // HEAD
    group_size = seq_local // MICRO
    row_count = group_size * stretch_len
    score_scale = HEAD ** (-0.5)
    ctx_place = lax.axis_index("ctx")
    own_stretch = jnp.sum(
        jnp.where(
            jnp.arange(stretch_order.shape[0], dtype=jnp.int32) == ctx_place, stretch_order, 0
        )
    )
    own_pos = own_stretch * stretch_len + jnp.arange(stretch_len, dtype=jnp.int32)
    all_segments = lax.all_gather(segments, "ctx", axis=1, tiled=True)

    def backward_micro(weights, kept_values, micro_index):
        (
            joint_full,
            mixer_full,
            expand_full,
            shrink_full,
            gain_one,
            shift_one,
            _,
            _,
            _,
            gain_two,
            shift_two,
            _,
            _,
        ) = weights
        (
            tokens,
            seg_local,
            seg_whole,
            normed,
            queries,
            keys_local,
            values_local,
            mixed_rows,
            attended,
            log_total,
            middle,
            second,
            expanded,
            active,
        ) = kept_values
        lower = micro_index * group_size
        tangent_rows = cotangent[lower : lower + group_size].reshape(row_count, model_width)
        active_grad = times_transposed(tangent_rows, shrink_full)
        gelu_pull = jax.vjp(lambda value_in: jax.nn.gelu(value_in, approximate=True), expanded)[1]
        expand_delta = gelu_pull(active_grad)[0].astype(jnp.bfloat16)
        second_grad = times_transposed(expand_delta, expand_full)
        mid_pull = jax.vjp(
            layer_norm, middle, gain_two.astype(jnp.float32), shift_two.astype(jnp.float32)
        )[1]
        middle_grad, gain_two_grad, shift_two_grad = mid_pull(second_grad)
        middle_grad = middle_grad + tangent_rows.astype(jnp.float32)
        branch_delta = middle_grad.astype(jnp.bfloat16)
        attended_delta = times_transposed(branch_delta, mixer_full).astype(jnp.bfloat16)
        grad_heads = attended_delta.reshape(group_size, stretch_len, head_count, HEAD)
        delta_heads = jnp.sum(
            grad_heads.transpose(0, 2, 1, 3).astype(jnp.float32) * attended, axis=-1
        )
        delta_rows = delta_heads.transpose(0, 2, 1)
        log_rows = log_total.transpose(0, 2, 1)
        lse_whole, delta_whole = (
            lax.all_gather(log_rows, "ctx", axis=1, tiled=True),
            lax.all_gather(delta_rows, "ctx", axis=1, tiled=True),
        )
        query_heads = queries.reshape(group_size, stretch_len, head_count, HEAD)
        key_heads = keys_local.reshape(group_size, stretch_len, head_count, HEAD)
        value_heads = values_local.reshape(group_size, stretch_len, head_count, HEAD)
        head_zeros = jnp.zeros((group_size, head_count, stretch_len, HEAD), jnp.float32)
        query_key_piece = lax.all_gather(keys_local, "ctx", axis=1, tiled=True)
        value_piece = lax.all_gather(values_local, "ctx", axis=1, tiled=True)
        count = query_key_piece.shape[1]
        step_len = piece_size(count)

        def query_block_step(turn_index, running):
            offset = turn_index * step_len
            key_block = lax.dynamic_slice_in_dim(query_key_piece, offset, step_len, 1).reshape(
                group_size, step_len, head_count, HEAD
            )
            value_block = lax.dynamic_slice_in_dim(value_piece, offset, step_len, 1).reshape(
                group_size, step_len, head_count, HEAD
            )
            key_pos = true_positions(stretch_order, offset, step_len, stretch_len)
            key_seg = lax.dynamic_slice_in_dim(seg_whole, offset, step_len, 1)
            allowed = (
                (seg_local[:, :, None] == key_seg[:, None, :])
                & (key_pos[None, None, :] <= own_pos[None, :, None])
            )[:, None]
            scores = (
                jnp.einsum(
                    "gqhd,gkhd->ghqk", query_heads, key_block, preferred_element_type=jnp.float32
                )
                * score_scale
            )
            probs = jnp.where(allowed, jnp.exp(scores - log_total[..., None]), 0.0)
            dots = jnp.einsum(
                "gqhd,gkhd->ghqk", grad_heads, value_block, preferred_element_type=jnp.float32
            )
            score_delta = (probs * (dots - delta_heads[..., None])).astype(jnp.bfloat16)
            return running + jnp.einsum(
                "ghqk,gkhd->ghqd", score_delta, key_block, preferred_element_type=jnp.float32
            )

        query_acc = lax.fori_loop(0, count // step_len, query_block_step, head_zeros)
        grad_rows3 = attended_delta.reshape(group_size, stretch_len, model_width)
        query_piece_rows = lax.all_gather(queries, "ctx", axis=1, tiled=True)
        grad_piece = lax.all_gather(grad_rows3, "ctx", axis=1, tiled=True)
        count = query_piece_rows.shape[1]
        key_step_len = piece_size(count)

        def key_block_step(turn_index, running):
            key_acc, value_acc = running
            offset = turn_index * key_step_len
            query_block = lax.dynamic_slice_in_dim(
                query_piece_rows, offset, key_step_len, 1
            ).reshape(group_size, key_step_len, head_count, HEAD)
            grad_block = lax.dynamic_slice_in_dim(grad_piece, offset, key_step_len, 1).reshape(
                group_size, key_step_len, head_count, HEAD
            )
            query_pos = true_positions(stretch_order, offset, key_step_len, stretch_len)
            query_seg = lax.dynamic_slice_in_dim(seg_whole, offset, key_step_len, 1)
            lse_block = lax.dynamic_slice_in_dim(lse_whole, offset, key_step_len, 1).transpose(
                0, 2, 1
            )
            delta_block = lax.dynamic_slice_in_dim(delta_whole, offset, key_step_len, 1).transpose(
                0, 2, 1
            )
            allowed = (
                (query_seg[:, :, None] == seg_local[:, None, :])
                & (own_pos[None, None, :] <= query_pos[None, :, None])
            )[:, None]
            scores = (
                jnp.einsum(
                    "gqhd,gkhd->ghqk", query_block, key_heads, preferred_element_type=jnp.float32
                )
                * score_scale
            )
            probs = jnp.where(allowed, jnp.exp(scores - lse_block[..., None]), 0.0)
            value_acc = value_acc + jnp.einsum(
                "ghqk,gqhd->ghkd",
                probs.astype(jnp.bfloat16),
                grad_block,
                preferred_element_type=jnp.float32,
            )
            dots = jnp.einsum(
                "gqhd,gkhd->ghqk", grad_block, value_heads, preferred_element_type=jnp.float32
            )
            score_delta = (probs * (dots - delta_block[..., None])).astype(jnp.bfloat16)
            key_acc = key_acc + jnp.einsum(
                "ghqk,gqhd->ghkd", score_delta, query_block, preferred_element_type=jnp.float32
            )
            return (key_acc, value_acc)

        key_acc, value_acc = lax.fori_loop(
            0, count // key_step_len, key_block_step, (head_zeros, head_zeros)
        )
        query_delta = (
            (query_acc * score_scale)
            .transpose(0, 2, 1, 3)
            .reshape(row_count, model_width)
            .astype(jnp.bfloat16)
        )
        key_delta = (
            (key_acc * score_scale)
            .transpose(0, 2, 1, 3)
            .reshape(row_count, model_width)
            .astype(jnp.bfloat16)
        )
        value_delta = (
            value_acc.transpose(0, 2, 1, 3).reshape(row_count, model_width).astype(jnp.bfloat16)
        )
        joint_delta = jnp.concatenate([query_delta, key_delta, value_delta], axis=1)
        normed_grad = times_transposed(joint_delta, joint_full)
        first_pull = jax.vjp(
            layer_norm,
            tokens.reshape(row_count, model_width),
            gain_one.astype(jnp.float32),
            shift_one.astype(jnp.float32),
        )[1]
        token_grad, gain_one_grad, shift_one_grad = first_pull(normed_grad)
        input_grad = (middle_grad + token_grad).reshape(group_size, stretch_len, model_width)
        small_terms = (
            gain_one_grad,
            shift_one_grad,
            jnp.sum(query_delta.astype(jnp.float32), axis=0),
            jnp.sum(value_delta.astype(jnp.float32), axis=0),
            jnp.sum(branch_delta.astype(jnp.float32), axis=0),
            gain_two_grad,
            shift_two_grad,
            jnp.sum(expand_delta.astype(jnp.float32), axis=0),
            jnp.sum(tangent_rows.astype(jnp.float32), axis=0),
        )
        factor_pairs = (
            normed.reshape(row_count, model_width),
            joint_delta,
            mixed_rows,
            branch_delta,
            second,
            expand_delta,
            active,
            tangent_rows,
        )
        return (input_grad, small_terms, factor_pairs)

    output_list = []
    input_list = []
    factor_list = []
    small_totals = None
    for micro_index in range(MICRO):
        forward_weights = fetch_weights(local_parts)
        (
            forward_joint_full,
            forward_mixer_full,
            forward_expand_full,
            forward_shrink_full,
            forward_gain_one,
            forward_shift_one,
            forward_qbias_full,
            forward_vbias_full,
            forward_mbias_full,
            forward_gain_two,
            forward_shift_two,
            forward_ebias_full,
            forward_sbias_full,
        ) = forward_weights
        forward_lower = micro_index * group_size
        forward_tokens = inputs[forward_lower : forward_lower + group_size].astype(jnp.float32)
        forward_seg_local = segments[forward_lower : forward_lower + group_size]
        forward_seg_whole = all_segments[forward_lower : forward_lower + group_size]
        forward_normed = layer_norm(
            forward_tokens,
            forward_gain_one.astype(jnp.float32),
            forward_shift_one.astype(jnp.float32),
        ).astype(jnp.bfloat16)
        joint_bias = jnp.concatenate(
            [forward_qbias_full, jnp.zeros_like(forward_qbias_full), forward_vbias_full]
        ).astype(jnp.float32)
        joint_rows = (
            jnp.dot(
                forward_normed.reshape(row_count, model_width),
                forward_joint_full,
                preferred_element_type=jnp.float32,
            )
            + joint_bias
        )
        joint_rows = joint_rows.astype(jnp.bfloat16).reshape(
            group_size, stretch_len, 3 * model_width
        )
        forward_queries = joint_rows[..., :model_width]
        forward_keys_local = joint_rows[..., model_width : 2 * model_width]
        forward_values_local = joint_rows[..., 2 * model_width :]
        forward_query_heads = forward_queries.reshape(group_size, stretch_len, head_count, HEAD)
        start_state = (
            jnp.full((group_size, head_count, stretch_len), masked_score, jnp.float32),
            jnp.zeros((group_size, head_count, stretch_len), jnp.float32),
            jnp.zeros((group_size, head_count, stretch_len, HEAD), jnp.float32),
        )
        forward_key_piece = lax.all_gather(forward_keys_local, "ctx", axis=1, tiled=True)
        forward_value_piece = lax.all_gather(forward_values_local, "ctx", axis=1, tiled=True)
        forward_count = forward_key_piece.shape[1]
        forward_step_len = piece_size(forward_count)

        def forward_block_step(turn_index, state):
            top_score, row_total, accumulated = state
            offset = turn_index * forward_step_len
            key_block = lax.dynamic_slice_in_dim(
                forward_key_piece, offset, forward_step_len, 1
            ).reshape(group_size, forward_step_len, head_count, HEAD)
            value_block = lax.dynamic_slice_in_dim(
                forward_value_piece, offset, forward_step_len, 1
            ).reshape(group_size, forward_step_len, head_count, HEAD)
            key_pos = true_positions(stretch_order, offset, forward_step_len, stretch_len)
            key_seg = lax.dynamic_slice_in_dim(forward_seg_whole, offset, forward_step_len, 1)
            allowed = (
                (forward_seg_local[:, :, None] == key_seg[:, None, :])
                & (key_pos[None, None, :] <= own_pos[None, :, None])
            )[:, None]
            scores = (
                jnp.einsum(
                    "gqhd,gkhd->ghqk",
                    forward_query_heads,
                    key_block,
                    preferred_element_type=jnp.float32,
                )
                * score_scale
            )
            scores = jnp.where(allowed, scores, masked_score)
            new_top = jnp.maximum(top_score, jnp.max(scores, axis=-1))
            weights_now = jnp.where(allowed, jnp.exp(scores - new_top[..., None]), 0.0)
            fade_factor = jnp.exp(top_score - new_top)
            row_total = row_total * fade_factor + jnp.sum(weights_now, axis=-1)
            accumulated = accumulated * fade_factor[..., None] + jnp.einsum(
                "ghqk,gkhd->ghqd",
                weights_now.astype(jnp.bfloat16),
                value_block,
                preferred_element_type=jnp.float32,
            )
            return (new_top, row_total, accumulated)

        top_score, row_total, accumulated = lax.fori_loop(
            0, forward_count // forward_step_len, forward_block_step, start_state
        )
        forward_attended = accumulated / row_total[..., None]
        forward_log_total = top_score + jnp.log(row_total)
        forward_mixed_rows = (
            forward_attended.transpose(0, 2, 1, 3)
            .reshape(row_count, model_width)
            .astype(jnp.bfloat16)
        )
        branch = jnp.dot(
            forward_mixed_rows, forward_mixer_full, preferred_element_type=jnp.float32
        ) + forward_mbias_full.astype(jnp.float32)
        forward_middle = forward_tokens.reshape(row_count, model_width) + branch
        forward_second = layer_norm(
            forward_middle,
            forward_gain_two.astype(jnp.float32),
            forward_shift_two.astype(jnp.float32),
        ).astype(jnp.bfloat16)
        forward_expanded = jnp.dot(
            forward_second, forward_expand_full, preferred_element_type=jnp.float32
        ) + forward_ebias_full.astype(jnp.float32)
        forward_active = jax.nn.gelu(forward_expanded, approximate=True).astype(jnp.bfloat16)
        output = (
            forward_middle
            + jnp.dot(forward_active, forward_shrink_full, preferred_element_type=jnp.float32)
            + forward_sbias_full.astype(jnp.float32)
        )
        forward_kept_values = (
            forward_tokens,
            forward_seg_local,
            forward_seg_whole,
            forward_normed,
            forward_queries,
            forward_keys_local,
            forward_values_local,
            forward_mixed_rows,
            forward_attended,
            forward_log_total,
            forward_middle,
            forward_second,
            forward_expanded,
            forward_active,
        )
        output_now = output.reshape(group_size, stretch_len, model_width).astype(jnp.bfloat16)
        kept_values = forward_kept_values
        backward_weights = fetch_weights(local_parts)
        input_now, small_terms, factor_pairs = backward_micro(
            backward_weights, kept_values, micro_index
        )
        output_list.append(output_now)
        input_list.append(input_now)
        factor_list.append(factor_pairs)
        if small_totals is None:
            small_totals = small_terms
        else:
            small_totals = tuple(
                (total_now + term_now for total_now, term_now in zip(small_totals, small_terms))
            )

    def joined(position):
        return jnp.concatenate([pairs_now[position] for pairs_now in factor_list], axis=0)

    matrices = (
        outer_sum(joined(0), joined(1)),
        outer_sum(joined(2), joined(3)),
        outer_sum(joined(4), joined(5)),
        outer_sum(joined(6), joined(7)),
    )
    reduced = reduce_gradients(matrices, small_totals)
    block_output = jnp.concatenate(output_list, axis=0)
    input_gradient = jnp.concatenate(input_list, axis=0)
    return (
        block_output,
        input_gradient,
        reduced[4],
        reduced[5],
        reduced[0],
        reduced[6],
        reduced[7],
        reduced[1],
        reduced[8],
        reduced[9],
        reduced[10],
        reduced[2],
        reduced[11],
        reduced[3],
        reduced[12],
    )


def joint_split(rows, parts, heads_each):
    count, three, width = rows.shape
    span = heads_each * HEAD
    slots = slot_width(heads_each)
    rows = jnp.pad(rows, ((0, 0), (0, 0), (0, parts * span - width)))
    rows = rows.reshape(count, three, parts, span)
    rows = jnp.pad(rows, ((0, 0), (0, 0), (0, 0), (0, slots - span)))
    return rows.transpose(2, 0, 1, 3).reshape(parts, count, three * slots)


def joint_join(pieces, heads_each, width):
    parts, count, wide = pieces.shape
    span = heads_each * HEAD
    rows = pieces.reshape(parts, count, 3, wide // 3)[..., :span]
    rows = rows.transpose(1, 2, 0, 3).reshape(count, 3, parts * span)
    return rows[..., :width].reshape(count, 3 * width)


def slot_width(heads_each):
    return -(-heads_each * HEAD // LANES) * LANES


def causal(k_block_is_diagonal, same):
    if k_block_is_diagonal:
        same = same & (
            lax.broadcasted_iota(jnp.int32, (TILE, TILE), 0)
            <= lax.broadcasted_iota(jnp.int32, (TILE, TILE), 1)
        )
    return same


def attend_forward_kernel(nf, nc, guests, *refs):
    n_in = sum(g[2] for g in guests)
    n_out = sum(g[3] for g in guests)
    own, ins, results, outs, own_scratch, scratch = split_refs(
        refs, (3, n_in, 3, n_out, 7, len(refs) - n_in - n_out - 13)
    )
    seg_row, seg_col, qkv_ref = own
    out_ref, turned_ref, lse_ref = results
    q_low, q_high, keys, values_turned, acc, tops, sums = own_scratch
    made = hosted(nf, nc, guests, ins, outs, scratch)
    greet_all(nc, {needs_of(g) for g in guests})
    begin_guests(made)
    send_guests(made)
    slots = out_ref.shape[1]
    scale = HEAD ** (-0.5)
    halves = (q_low, q_high)

    def one_block(q_block, k_block, first):
        q_at = pl.ds(pl.multiple_of(q_block * TILE, TILE), TILE)
        k_at = pl.ds(pl.multiple_of(k_block * TILE, TILE), TILE)
        same = causal(first, seg_col[k_at, :] == seg_row[:, q_at])
        for half in range(2):
            dims = pl.ds(half * HEAD, HEAD)
            scores = times_transposed(keys[k_at, :], halves[half][q_at, :])
            scores = jnp.where(same, scores, masked_score)
            top = jnp.max(scores, axis=0, keepdims=True)
            if not first:
                old_top = tops[half]
                top = jnp.maximum(old_top, top)
            weights = jnp.exp(scores - top)
            total = jnp.sum(weights, axis=0, keepdims=True)
            part = jnp.dot(
                values_turned[dims, k_at],
                weights.astype(jnp.bfloat16),
                preferred_element_type=jnp.float32,
            )
            if not first:
                fade = jnp.exp(old_top - top)
                total = total + sums[half] * fade
                part = part + acc[dims, :] * fade
            tops[half] = top
            sums[half] = total
            acc[dims, :] = part

    @pl.loop(0, slots // LANES)
    def _(pair):
        column = pl.multiple_of(pair * LANES, LANES)
        queries = qkv_ref[:, pl.ds(column, LANES)] * jnp.bfloat16(scale)
        low_half = lax.broadcasted_iota(jnp.int32, queries.shape, 1) < HEAD
        q_low[...] = jnp.where(low_half, queries, jnp.zeros_like(queries))
        q_high[...] = jnp.where(low_half, jnp.zeros_like(queries), queries)
        keys[...] = qkv_ref[:, pl.ds(slots + column, LANES)]
        values = qkv_ref[:, pl.ds(2 * slots + column, LANES)]
        values_turned[...] = values.astype(jnp.float32).T.astype(jnp.bfloat16)

        @pl.loop(0, qkv_ref.shape[0] // TILE)
        def _(q_block):
            one_block(q_block, q_block, True)

            @pl.loop(0, q_block)
            def _(k_block):
                one_block(q_block, k_block, False)

            q_at = pl.ds(pl.multiple_of(q_block * TILE, TILE), TILE)
            for half in range(2):
                dims = pl.ds(half * HEAD, HEAD)
                acc[dims, :] = acc[dims, :] / sums[half]
                lse_ref[pair, pl.ds(half, 1), q_at] = tops[half] + jnp.log(sums[half])
            turned_ref[pair, :, q_at] = acc[...]
            out_ref[q_at, pl.ds(column, LANES)] = acc[...].T.astype(jnp.bfloat16)

        @pl.when(pair == 2)
        def _():
            pass_on_guests(made)

    run_guests(made)


def attend_backward_kernel(nf, nc, guests, *refs):
    n_in = sum(g[2] for g in guests)
    n_out = sum(g[3] for g in guests)
    own, ins, results, outs, own_scratch, scratch = split_refs(
        refs, (6, n_in, 1, n_out, 11, len(refs) - n_in - n_out - 18)
    )
    seg_row, seg_col, qkv_ref, grad_ref, turned_ref, lse_ref = own
    out_ref = results[0]
    (
        q_low, q_high, keys, keys_turned, values, g_low, g_high,
        query_acc, key_acc, value_acc, corrections,
    ) = own_scratch
    made = hosted(nf, nc, guests, ins, outs, scratch)
    greet_all(nc, {needs_of(g) for g in guests})
    begin_guests(made)
    slots = grad_ref.shape[1]
    scale = HEAD ** (-0.5)
    q_halves = (q_low, q_high)
    g_halves = (g_low, g_high)

    def one_block(pair, q_block, k_block, first):
        q_at = pl.ds(pl.multiple_of(q_block * TILE, TILE), TILE)
        k_at = pl.ds(pl.multiple_of(k_block * TILE, TILE), TILE)
        same = causal(first, seg_col[k_at, :] == seg_row[:, q_at])
        value_sum = value_acc[k_at, :]
        key_sum = key_acc[k_at, :]
        for half in range(2):
            dims = pl.ds(half * HEAD, HEAD)
            query_rows = q_halves[half][q_at, :]
            grad_rows = g_halves[half][q_at, :]
            scores = times_transposed(keys[k_at, :], query_rows)
            lse = lse_ref[pair, pl.ds(half, 1), q_at]
            probs = jnp.exp(jnp.where(same, scores - lse, masked_score))
            dots = times_transposed(values[k_at, :], grad_rows)
            delta = (probs * (dots - corrections[half, :, q_at])).astype(jnp.bfloat16)
            value_sum = value_sum + jnp.dot(
                probs.astype(jnp.bfloat16), grad_rows, preferred_element_type=jnp.float32
            )
            key_sum = key_sum + jnp.dot(delta, query_rows, preferred_element_type=jnp.float32)
            part = jnp.dot(keys_turned[dims, k_at], delta, preferred_element_type=jnp.float32)
            if first:
                query_acc[dims, :] = part
            else:
                query_acc[dims, :] += part
        value_acc[k_at, :] = value_sum
        key_acc[k_at, :] = key_sum

    @pl.loop(0, slots // LANES)
    def _(pair):
        column = pl.multiple_of(pair * LANES, LANES)
        queries = qkv_ref[:, pl.ds(column, LANES)] * jnp.bfloat16(scale)
        low_half = lax.broadcasted_iota(jnp.int32, queries.shape, 1) < HEAD
        zeros = jnp.zeros_like(queries)
        q_low[...] = jnp.where(low_half, queries, zeros)
        q_high[...] = jnp.where(low_half, zeros, queries)
        grads = grad_ref[:, pl.ds(column, LANES)]
        g_low[...] = jnp.where(low_half, grads, zeros)
        g_high[...] = jnp.where(low_half, zeros, grads)
        product = grads.astype(jnp.float32).T * turned_ref[pair]
        corrections[0] = jnp.sum(product[:HEAD], axis=0, keepdims=True)
        corrections[1] = jnp.sum(product[HEAD:], axis=0, keepdims=True)
        keys_now = qkv_ref[:, pl.ds(slots + column, LANES)]
        keys[...] = keys_now
        keys_turned[...] = keys_now.astype(jnp.float32).T.astype(jnp.bfloat16)
        values[...] = qkv_ref[:, pl.ds(2 * slots + column, LANES)]
        key_acc[...] = jnp.zeros_like(key_acc)
        value_acc[...] = jnp.zeros_like(value_acc)

        @pl.loop(0, qkv_ref.shape[0] // TILE)
        def _(q_block):
            one_block(pair, q_block, q_block, True)

            @pl.loop(0, q_block)
            def _(k_block):
                one_block(pair, q_block, k_block, False)

            q_at = pl.ds(pl.multiple_of(q_block * TILE, TILE), TILE)
            out_ref[q_at, pl.ds(column, LANES)] = (query_acc[...].T * scale).astype(jnp.bfloat16)

        out_ref[:, pl.ds(slots + column, LANES)] = key_acc[...].astype(jnp.bfloat16)
        out_ref[:, pl.ds(2 * slots + column, LANES)] = value_acc[...].astype(jnp.bfloat16)

        @pl.when(pair == 0)
        def _():
            send_guests(made)

    run_guests(made)


def pick(blocks, order):
    return blocks.at[order].get(mode="promise_in_bounds", unique_indices=True)


def all_units(vector, nc, nf, unit_each, shard):
    vector = vector.transpose(1, 0, 2).reshape(nc, nf, unit_each)
    return lax.dynamic_index_in_dim(vector, shard, 1, keepdims=False).reshape(nc * unit_each)


def rows_of(vectors, count):
    row = jnp.arange(count, dtype=jnp.int32)[:, None]
    total = jnp.where(row == 0, vectors[0][None], jnp.zeros_like(vectors[0][None]))
    for k, vector in enumerate(vectors[1:], 1):
        total = jnp.where(row == k, vector[None], total)
    return total


def normalize(rows):
    center = rows - jnp.mean(rows, axis=-1, keepdims=True)
    spread = jnp.mean(center * center, axis=-1, keepdims=True)
    inverse = lax.rsqrt(spread + epsilon)
    return center * inverse, inverse


def normalize_back(grads, gain, unit, inverse):
    pulled = grads * gain
    return inverse * (
        pulled
        - jnp.mean(pulled, axis=-1, keepdims=True)
        - unit * jnp.mean(pulled * unit, axis=-1, keepdims=True)
    )


def gelu_parts(value):
    root = 0.7978845608028654
    inner = root * (value + 0.044715 * value * value * value)
    bend = jnp.tanh(inner)
    slope = 0.5 * (1.0 + bend) + 0.5 * value * (1.0 - bend * bend) * root * (
        1.0 + 3 * 0.044715 * value * value
    )
    return 0.5 * value * (1.0 + bend), slope


def mesh_copy(source, target, send, receive, device):
    return pltpu.make_async_remote_copy(
        src_ref=source,
        dst_ref=target,
        send_sem=send,
        recv_sem=receive,
        device_id=device,
        device_id_type=pl.DeviceIdType.MESH,
    )


def greet(devices, swaps=()):
    barrier = pltpu.get_barrier_semaphore()
    for device in devices:
        pl.semaphore_signal(
            barrier, inc=1, device_id=device, device_id_type=pl.DeviceIdType.MESH
        )
    for device in swaps:

        @pl.when(elsewhere(device))
        def _():
            pl.semaphore_signal(
                barrier, inc=1, device_id=device, device_id_type=pl.DeviceIdType.MESH
            )

    count = len(devices)
    for device in swaps:
        count = count + jnp.where(elsewhere(device), 1, 0)
    pl.semaphore_wait(barrier, count)


def elsewhere(device):
    apart = (device[0] - lax.axis_index("fsdp")) * 64 + device[1] - lax.axis_index("ctx")
    return apart != 0


def to_column(f, c, i):
    return 2 * (c // 2 % 2) + c % 2, 2 * (2 * i + f % 2) + (f // 2 + f % 2) % 2, c // 4


def to_origin(f, c, j):
    core = c // 2 % 2
    return 2 * ((c % 2 + core) % 2) + core, 2 * (2 * j + f // 2) + f % 2, c // 4


def swap_peers(move, back):
    f, c = lax.axis_index("fsdp"), lax.axis_index("ctx")
    return [way(f, c, k)[:2] for way in (move, back) for k in range(2)]


def ctx_peers(nc):
    f, c = lax.axis_index("fsdp"), lax.axis_index("ctx")
    return [(f, (c + k) % nc) for k in range(1, nc)]


def greet_all(nc, needs):
    devices, swaps = [], []
    if "fsdp" in needs:
        devices += fsdp_peers(3)
    elif "near" in needs:
        devices += fsdp_peers(2)
    if "ctx" in needs:
        devices += ctx_peers(nc)
    elif "ring" in needs:
        devices += ring_peers(nc)
    if "column" in needs:
        swaps += swap_peers(to_column, to_origin)
    if "origin" in needs:
        swaps += swap_peers(to_origin, to_column)
    greet(devices, swaps)


def fsdp_places():
    shard = lax.axis_index("fsdp")
    partner = shard + 1 - 2 * (shard % 2)
    return shard, partner, (shard + 2) % 4, (partner + 2) % 4


def ring_places(nc):
    place = lax.axis_index("ctx")
    z, y = place // 2, place % 2
    spot = z * (1 - y) + (nc - 1 - z) * y

    def holder(at):
        at = (at + nc) % nc
        side = at // (nc // 2)
        return (1 - side) * 2 * at + side * (2 * (nc - 1 - at) + 1)

    return spot, holder


def ring_peers(nc):
    spot, holder = ring_places(nc)
    shard = lax.axis_index("fsdp")
    return [(shard, holder(spot + way)) for way in (1, -1)]


def fsdp_peers(count):
    place = lax.axis_index("ctx")
    return [(at, place) for at in fsdp_places()[1 : 1 + count]]


def chunks_of(rows, count):
    step = -(-rows // count // 16) * 16
    return [(at, min(step, rows - at)) for at in range(0, rows, step)]


def row_step(size):
    return next(step for step in (56, 40, 32, 16, 8) if size % step == 0)


class FsdpGather:
    SEMS = (7, 4)

    def __init__(self, own, out, sems):
        self.own, self.out, self.sems = own, out, sems
        self.shard, self.partner, self.cross, self.corner = fsdp_places()
        self.place = lax.axis_index("ctx")
        self.chunks = chunks_of(own.shape[0], 4)

    def copy(self, kind, k):
        at, size = self.chunks[k]
        rows = pl.ds(at, size)
        if kind == "own":
            return pltpu.make_async_copy(
                self.own.at[rows], self.out.at[self.shard, rows], self.sems.at[6, k]
            )
        if kind == "across":
            source, slot, device, sem = self.own.at[rows], self.shard, self.cross, 0
        elif kind == "beside":
            source, slot, device, sem = self.own.at[rows], self.shard, self.partner, 2
        else:
            slot, device, sem = self.cross, self.partner, 4
            source = self.out.at[slot, rows]
        return mesh_copy(
            source,
            self.out.at[slot, rows],
            self.sems.at[sem, k],
            self.sems.at[sem + 1, k],
            (device, self.place),
        )

    def begin(self):
        for kind in ("across", "beside", "own"):
            for k in range(len(self.chunks)):
                self.copy(kind, k).start()

    def pass_on(self):
        for k in range(len(self.chunks)):
            self.copy("across", k).wait_recv()
            self.copy("on", k).start()

    def finish(self):
        for k in range(len(self.chunks)):
            self.copy("across", k).wait_send()
            self.copy("beside", k).wait()
            self.copy("on", k).wait()
            self.copy("own", k).wait()


def joint_parts(nf, nc, rows, depth, place):
    thin = depth // nf // (8 * nc) * 8
    rest, each = rows - nf * thin, nc // nf
    parts = []
    for f in range(nf):
        parts.append((f * thin, pl.multiple_of(f * (depth // nf) + place * thin, 8), thin))
    last = (place // each) * (depth // nf) + nc * thin + (place % each) * rest
    parts.append((nf * thin, pl.multiple_of(last, 8), rest))
    return parts


def half_of(parts, way):
    middle = (len(parts) - 1) // 2
    return parts[:middle] if way == 1 else parts[middle:]


class RingGather:
    def __init__(self, nc, own, out, sems, parts=None):
        self.nc, self.own, self.out, self.sems = nc, own, out, sems
        self.spot, self.holder = ring_places(nc)
        self.shard = lax.axis_index("fsdp")
        self.parts = parts
        if parts is None:
            self.rows = out.shape[1]
            self.half = self.rows // 2 // 8 * 8

    def pieces(self, origin, way, step):
        if self.parts is not None:
            parts = self.parts(origin)
            if step == self.nc // 2:
                parts = half_of(parts, way)
            return [(pl.ds(at, size), self.out.at[pl.ds(there, size)]) for at, there, size in parts]
        rows = pl.ds(0, self.rows)
        if step == self.nc // 2:
            rows = pl.ds(0, self.half) if way == 1 else pl.ds(self.half, self.rows - self.half)
        return [(rows, self.out.at[origin, rows])]

    def copies(self, way, step):
        origin = self.holder(self.spot - way * (step - 1))
        side = 0 if way == 1 else 2
        made = []
        for k, (rows, whole) in enumerate(self.pieces(origin, way, step)):
            made.append(
                mesh_copy(
                    self.own.at[rows] if step == 1 else whole,
                    whole,
                    self.sems.at[side, step - 1, k],
                    self.sems.at[side + 1, step - 1, k],
                    (self.shard, self.holder(self.spot + way)),
                )
            )
        return made

    def keeps(self):
        return [
            pltpu.make_async_copy(self.own.at[rows], whole, self.sems.at[4, 0, k])
            for k, (rows, whole) in enumerate(self.pieces(lax.axis_index("ctx"), 1, 1))
        ]

    def start(self, step):
        for way in (1, -1):
            for copy in self.copies(way, step):
                copy.start()
        if step == 1:
            for copy in self.keeps():
                copy.start()

    def arrived(self, way, step):
        for copy in self.copies(way, step):
            copy.wait_recv()

    def advance(self, step):
        for way in (1, -1):
            self.arrived(way, step - 1)
            for copy in self.copies(way, step):
                copy.start()

    def finish(self, first, last):
        for way in (1, -1):
            for step in range(first, last + 1):
                for copy in self.copies(way, step):
                    copy.wait_send()
            self.arrived(way, last)
        if first == 1:
            for copy in self.keeps():
                copy.wait()


class RingScatter:
    def __init__(self, nc, mine, out, right, left, sems, parts=None):
        self.nc, self.mine, self.out, self.sems = nc, mine, out, sems
        self.inbox = {1: right, -1: left}
        self.spot, self.holder = ring_places(nc)
        self.shard = lax.axis_index("fsdp")
        self.rows = out.shape[0]
        self.half = self.rows // 2 // 8 * 8
        self.parts = parts

    def copies(self, way, step):
        inbox = self.inbox[way]
        if step > 1:
            sources = [(pl.ds(0, self.rows), inbox.at[step - 2])]
        else:
            place = self.holder(self.spot + self.nc // 2)
            if self.parts is not None:
                sources = [
                    (pl.ds(at, size), self.mine.at[pl.ds(there, size)])
                    for at, there, size in half_of(self.parts(place), way)
                ]
            else:
                low, high = pl.ds(0, self.half), pl.ds(self.half, self.rows - self.half)
                rows = low if way == 1 else high
                sources = [(rows, self.mine.at[place, rows])]
        side = 0 if way == 1 else 2
        return [
            mesh_copy(
                source,
                inbox.at[step - 1, rows],
                self.sems.at[side, step - 1, k],
                self.sems.at[side + 1, step - 1, k],
                (self.shard, self.holder(self.spot + way)),
            )
            for k, (rows, source) in enumerate(sources)
        ]

    def begin(self):
        for way in (1, -1):
            for copy in self.copies(way, 1):
                copy.start()

    def advance(self, step):
        for way in (1, -1):
            for copy in self.copies(way, step - 1):
                copy.wait_recv()
            box = self.inbox[way].at[step - 2]
            place = self.holder(self.spot + way * (self.nc // 2 + 1 - step))
            if self.parts is not None:
                parts = self.parts(place)
                came = half_of(parts, way) if step == 2 else parts
                for part in parts:
                    at, there, size = part
                    target, source = box.at[pl.ds(at, size)], self.mine.at[pl.ds(there, size)]
                    if any(part is other for other in came):
                        add_rows(target, source, (0, size))
                    else:
                        set_rows(target, source, (0, size))
            else:
                join_rows(box, self.mine.at[place], step, way, self.rows, self.half)
            for copy in self.copies(way, step):
                copy.start()

    def finish(self):
        last = self.nc // 2
        for way in (1, -1):
            for copy in self.copies(way, last):
                copy.wait_recv()
        right, left = self.inbox[1].at[last - 1], self.inbox[-1].at[last - 1]
        place = lax.axis_index("ctx")
        if self.parts is not None:
            for at, there, size in self.parts(place):
                rows = pl.ds(at, size)
                sum_rows(
                    self.out.at[rows], self.mine.at[pl.ds(there, size)], right.at[rows], left.at[rows]
                )
        else:
            sum_rows(self.out, self.mine.at[place], right, left)
        for way in (1, -1):
            for step in range(1, last + 1):
                for copy in self.copies(way, step):
                    copy.wait_send()


def join_rows(box, mine, step, way, rows, half):
    low, high = (0, half), (half, rows - half)
    if step == 2:
        got, rest = (low, high) if way == 1 else (high, low)
        set_rows(box, mine, rest)
    else:
        got = (0, rows)
    add_rows(box, mine, got)


def add_rows(target, source, rows):
    first, size = rows
    step = row_step(size)

    @pl.loop(0, size // step)
    def _(turn):
        at = pl.ds(pl.multiple_of(first + turn * step, 8), step)
        target[at] = (target[at].astype(jnp.float32) + source[at].astype(jnp.float32)).astype(
            target.dtype
        )


def set_rows(target, source, rows):
    first, size = rows
    step = row_step(size)

    @pl.loop(0, size // step)
    def _(turn):
        at = pl.ds(pl.multiple_of(first + turn * step, 8), step)
        target[at] = source[at]


def sum_rows(out, mine, right, left):
    step = row_step(out.shape[0])

    @pl.loop(0, out.shape[0] // step)
    def _(turn):
        at = pl.ds(pl.multiple_of(turn * step, 8), step)
        out[at] = (
            mine[at].astype(jnp.float32)
            + right[at].astype(jnp.float32)
            + left[at].astype(jnp.float32)
        ).astype(out.dtype)


class GatherStep:
    NEEDS = "ring"
    VMEM_IN = 0

    def __init__(self, nf, nc, step, ins, outs, scratch):
        self.step = step
        self.ring = RingGather(nc, None, outs[0], scratch[0])

    @staticmethod
    def shapes(nf, nc, step, arrays):
        (whole,) = arrays
        return (
            [jax.ShapeDtypeStruct(whole.shape, whole.dtype)],
            [pltpu.SemaphoreType.DMA((5, nc // 2, 1))],
            True,
        )

    def begin(self):
        self.ring.start(self.step)

    def send(self):
        pass

    def finish(self):
        self.ring.finish(self.step, self.step)


class SideGather:
    NEEDS = "near"
    VMEM_IN = 1

    def __init__(self, nf, nc, step, ins, outs, scratch):
        self.side = FsdpGather(ins[0], outs[0], scratch[0])

    @staticmethod
    def shapes(nf, nc, step, arrays):
        (array,) = arrays
        return (
            [jax.ShapeDtypeStruct((nf,) + array.shape, array.dtype)],
            [pltpu.SemaphoreType.DMA(FsdpGather.SEMS)],
            False,
        )

    def begin(self):
        pass

    def send(self):
        self.side.begin()

    def finish(self):
        self.side.finish()


class ScatterRing:
    NEEDS = "ring"
    VMEM_IN = 1

    def __init__(self, nf, nc, step, ins, outs, scratch):
        right, left, total, self.put_sem, sems = scratch
        self.out, self.total = outs[0], total
        parts = None
        if step:
            parts = functools.partial(joint_parts, nf, nc, step, ins[0].shape[0])
        self.ring = RingScatter(nc, ins[0], total, right, left, sems, parts)

    @staticmethod
    def shapes(nf, nc, step, arrays):
        mine = arrays[0]
        shape = (step,) + mine.shape[1:] if step else mine.shape[1:]
        box = pltpu.VMEM((nc // 2,) + shape, mine.dtype)
        return (
            [jax.ShapeDtypeStruct(shape, mine.dtype)],
            [
                box,
                box,
                pltpu.VMEM(shape, mine.dtype),
                pltpu.SemaphoreType.DMA((1,)),
                pltpu.SemaphoreType.DMA((4, nc // 2, nf + 1)),
            ],
            False,
        )

    def begin(self):
        self.ring.begin()

    def send(self):
        self.ring.advance(2)

    def more(self, step):
        self.ring.advance(step)

    def finish(self):
        self.ring.finish()
        put = pltpu.make_async_copy(self.total, self.out, self.put_sem.at[0])
        put.start()
        put.wait()


class ScatterStep:
    NEEDS = "ring"
    VMEM_IN = 0

    def __init__(self, nf, nc, step, ins, outs, scratch):
        self.nc, self.step = nc, step
        self.mine, self.before, self.outs = ins[0], ins[1:], outs
        self.sems = scratch[-1]
        self.boxes = scratch[:-1]
        self.spot, self.holder = ring_places(nc)
        self.shard = lax.axis_index("fsdp")
        self.rows = outs[0].shape[0]
        self.half = self.rows // 2 // 8 * 8

    @staticmethod
    def shapes(nf, nc, step, arrays):
        mine = arrays[0]
        block = jax.ShapeDtypeStruct(mine.shape[1:], mine.dtype)
        outs = [block, block]
        scratch = []
        if step > 1:
            scratch += [pltpu.VMEM(mine.shape[1:], mine.dtype)] * 4
        return outs, scratch + [pltpu.SemaphoreType.DMA((4, 4))], False

    def copy(self, k):
        way = (1, -1)[k]
        rows = pl.ds(0, self.rows)
        if self.step == 1:
            rows = pl.ds(0, self.half) if way == 1 else pl.ds(self.half, self.rows - self.half)
            source = self.mine.at[self.holder(self.spot + self.nc // 2), rows]
        else:
            source = self.boxes[k]
        return mesh_copy(
            source,
            self.outs[k].at[rows],
            self.sems.at[0, k],
            self.sems.at[1, k],
            (self.shard, self.holder(self.spot + way)),
        )

    def loads(self, k):
        way = (1, -1)[k]
        rows = pl.ds(0, self.rows)
        if self.step == 2:
            rows = pl.ds(0, self.half) if way == 1 else pl.ds(self.half, self.rows - self.half)
        place = self.holder(self.spot + way * (self.nc // 2 + 1 - self.step))
        return [
            pltpu.make_async_copy(
                self.before[k].at[rows], self.boxes[k].at[rows], self.sems.at[2, k]
            ),
            pltpu.make_async_copy(self.mine.at[place], self.boxes[2 + k], self.sems.at[3, k]),
        ]

    def begin(self):
        for k in range(2):
            if self.step == 1:
                self.copy(k).start()
            else:
                for load in self.loads(k):
                    load.start()

    def send(self):
        if self.step > 1:
            for k in range(2):
                for load in self.loads(k):
                    load.wait()
                way = (1, -1)[k]
                join_rows(self.boxes[k], self.boxes[2 + k], self.step, way, self.rows, self.half)
                self.copy(k).start()

    def finish(self):
        for k in range(2):
            self.copy(k).wait()


class Trade:
    def __init__(self, axis, size, source, target, sems, hops=None):
        self.axis, self.size = axis, size
        self.hops = hops or tuple(range(1, size))
        self.source, self.target, self.sems = source, target, sems
        self.me = lax.axis_index(axis)

    def copies(self):
        made = []
        for k in self.hops:
            other = (self.me + k) % self.size
            device = (
                (other, lax.axis_index("ctx"))
                if self.axis == "fsdp"
                else (lax.axis_index("fsdp"), other)
            )
            made.append(
                mesh_copy(
                    self.source(other),
                    self.target(self.me),
                    self.sems.at[0, k],
                    self.sems.at[1, k],
                    device,
                )
            )
        made.append(
            pltpu.make_async_copy(
                self.source(self.me), self.target(self.me), self.sems.at[2, 0]
            )
        )
        return made

    def begin(self):
        for copy in self.copies():
            copy.start()

    def finish(self):
        for copy in self.copies():
            copy.wait()


class TradeGuest:
    VMEM_IN = 1

    def __init__(self, nf, nc, step, ins, outs, scratch):
        axis, hops = step
        size = nf if axis == "fsdp" else nc
        whole = len(ins[0].shape) < len(outs[0].shape)
        self.trade = Trade(
            axis,
            size,
            (lambda k: ins[0]) if whole else (lambda k: ins[0].at[k]),
            lambda k: outs[0].at[k],
            scratch[0],
            hops,
        )

    @staticmethod
    def shapes(nf, nc, step, arrays):
        (array,) = arrays
        size = nf if step[0] == "fsdp" else nc
        shape = array.shape if array.ndim == 3 else (size,) + array.shape
        return (
            [jax.ShapeDtypeStruct(shape, array.dtype)],
            [pltpu.SemaphoreType.DMA((3, size))],
            False,
        )

    def begin(self):
        pass

    def send(self):
        self.trade.begin()

    def finish(self):
        self.trade.finish()


class SwapGuest:
    VMEM_IN = 1

    def __init__(self, nf, nc, step, ins, outs, scratch):
        self.blocks, self.out, self.sems = ins[0], outs[0], scratch[0]
        self.move, self.back = (
            (to_column, to_origin) if step == "column" else (to_origin, to_column)
        )

    @staticmethod
    def shapes(nf, nc, step, arrays):
        (array,) = arrays
        return (
            [jax.ShapeDtypeStruct(array.shape, array.dtype)],
            [pltpu.SemaphoreType.DMA((3, 2))],
            False,
        )

    def copies(self, k):
        f, c = lax.axis_index("fsdp"), lax.axis_index("ctx")
        there = self.move(f, c, k)
        source, target = self.blocks.at[k], self.out.at[there[2]]
        away = mesh_copy(
            source, target, self.sems.at[0, k], self.sems.at[1, there[2]], there[:2]
        )
        return elsewhere(there), away, pltpu.make_async_copy(source, target, self.sems.at[2, k])

    def begin(self):
        pass

    def send(self):
        for k in range(2):
            apart, away, stay = self.copies(k)

            @pl.when(apart)
            def _():
                away.start()

            @pl.when(jnp.logical_not(apart))
            def _():
                stay.start()

    def finish(self):
        f, c = lax.axis_index("fsdp"), lax.axis_index("ctx")
        for k in range(2):
            apart, away, stay = self.copies(k)

            @pl.when(apart)
            def _():
                away.wait_send()

            @pl.when(jnp.logical_not(apart))
            def _():
                stay.wait()

            origin = self.back(f, c, k)
            arrival = mesh_copy(
                self.blocks.at[0],
                self.out.at[k],
                self.sems.at[0, 0],
                self.sems.at[1, k],
                origin[:2],
            )

            @pl.when(elsewhere(origin))
            def _():
                arrival.wait_recv()


def begin_guests(made):
    for guest in made:
        guest.begin()
    early_guests(made)


def early_guests(made):
    for guest in made:
        if isinstance(guest, ScatterStep):
            guest.send()


def send_guests(made):
    for guest in made:
        if not isinstance(guest, ScatterStep):
            guest.send()


def pass_on_guests(made):
    for guest in made:
        if isinstance(guest, SideGather):
            guest.side.pass_on()


def needs_of(guest):
    kind, step = guest[0], guest[1]
    if kind is TradeGuest:
        return step[0]
    if kind is SwapGuest:
        return step
    return kind.NEEDS


def split_refs(refs, counts):
    parts, at = [], 0
    for count in counts:
        parts.append(refs[at : at + count])
        at += count
    return parts


def hosted(nf, nc, guests, ins, outs, scratch):
    made, a, b, c = [], 0, 0, 0
    for kind, step, n_in, n_out, n_scratch in guests:
        made.append(
            kind(nf, nc, step, ins[a : a + n_in], outs[b : b + n_out], scratch[c : c + n_scratch])
        )
        a, b, c = a + n_in, b + n_out, c + n_scratch
    return made


def run_guests(made):
    for step in (3, 4):
        for guest in made:
            if isinstance(guest, ScatterRing):
                guest.more(step)
    for guest in made:
        guest.finish()


def lone_kernel(nf, nc, guests, *refs):
    n_in = sum(g[2] for g in guests)
    n_out = sum(g[3] for g in guests)
    ins, outs, scratch = split_refs(refs, (n_in, n_out, len(refs) - n_in - n_out))
    made = hosted(nf, nc, guests, ins, outs, scratch)
    greet_all(nc, {needs_of(g) for g in guests})
    begin_guests(made)
    send_guests(made)
    run_guests(made)


def gather_fsdp_kernel(nf, nc, guests, *refs):
    n_in = sum(g[2] for g in guests)
    n_out = sum(g[3] for g in guests)
    own, ins, out, outs, sems, scratch = split_refs(
        refs, (1, n_in, 1, n_out, 1, len(refs) - n_in - n_out - 3)
    )
    side = FsdpGather(own[0], out[0], sems[0])
    made = hosted(nf, nc, guests, ins, outs, scratch)
    greet_all(nc, {"near"} | {needs_of(g) for g in guests})
    side.begin()
    begin_guests(made)
    send_guests(made)
    side.pass_on()
    side.finish()
    run_guests(made)


def scatter_fsdp_kernel(nf, nc, guests, turned, *refs):
    n_in = sum(g[2] for g in guests)
    n_out = sum(g[3] for g in guests)
    operands, ins, result, outs, own_scratch, scratch = split_refs(
        refs, (2, n_in, 1, n_out, 6, len(refs) - n_in - n_out - 9)
    )
    left_ref, right_ref = operands
    out_ref = result[0]
    part_ref, first_in, own_in, chip_sum, across_in, sems = own_scratch
    shard, partner, cross, corner = fsdp_places()
    place = lax.axis_index("ctx")
    made = hosted(nf, nc, guests, ins, outs, scratch)
    greet_all(nc, {"near"} | {needs_of(g) for g in guests})
    for guest in made:
        guest.begin()
    count, width = out_ref.shape
    chunks = chunks_of(count, 4)

    def copy(kind, k):
        at, size = chunks[k]
        rows = pl.ds(at, size)
        if kind == 0:
            source, target, device = part_ref.at[corner, rows], first_in, partner
        elif kind == 1:
            source, target, device = part_ref.at[partner, rows], own_in, partner
        else:
            source, target, device = chip_sum.at[rows], across_in, cross
        return mesh_copy(
            source,
            target.at[rows],
            sems.at[2 * kind, k],
            sems.at[2 * kind + 1, k],
            (device, place),
        )

    half = count // 2
    early, late = chunks[: len(chunks) // 2], chunks[len(chunks) // 2 :]

    def add_and_send(first, some):
        for k, (at, size) in enumerate(some, first):
            copy(0, k).wait_recv()

            @pl.loop(0, size // 32)
            def _(step):
                rows = pl.ds(pl.multiple_of(at + step * 32, 32), 32)
                chip_sum[rows] = (
                    part_ref[cross, rows].astype(jnp.float32)
                    + first_in[rows].astype(jnp.float32)
                ).astype(chip_sum.dtype)

            copy(2, k).start()

    @pl.loop(0, 8)
    def _(turn):
        pair = turn // 4
        of_two = (turn % 2) * (1 - pair) + (turn // 2 % 2) * pair
        upper = (turn // 2 % 2) * (1 - pair) + (turn % 2) * pair
        base = partner * (1 - of_two) + shard * of_two
        block = (base + 2 * (1 - pair)) % 4
        start = pl.multiple_of(upper * half, half)
        rows = left_ref[pl.ds(pl.multiple_of(block * count + start, half), half), :]
        for at in range(0, width, 512):
            size = 512 if at + 1024 <= width else width - at
            if turned:
                piece = times_transposed(rows, right_ref[at : at + size, :])
            else:
                piece = jnp.dot(
                    rows, right_ref[:, at : at + size], preferred_element_type=jnp.float32
                )
            part_ref[block, pl.ds(start, half), at : at + size] = piece.astype(part_ref.dtype)
            if at + size == width:
                break

        @pl.when(turn == 0)
        def _():
            for k in range(len(early)):
                copy(0, k).start()
            early_guests(made)

        @pl.when(turn == 1)
        def _():
            add_and_send(0, early)

        @pl.when(turn == 2)
        def _():
            for k in range(len(early), len(chunks)):
                copy(0, k).start()

        @pl.when(turn == 3)
        def _():
            add_and_send(len(early), late)
            send_guests(made)

        @pl.when(turn == 5)
        def _():
            for k in range(len(chunks)):
                copy(1, k).start()

    for k, (at, size) in enumerate(chunks):
        copy(1, k).wait_recv()
        copy(2, k).wait_recv()

        @pl.loop(0, size // 32)
        def _(turn):
            rows = pl.ds(pl.multiple_of(at + turn * 32, 32), 32)
            out_ref[rows] = (
                part_ref[shard, rows].astype(jnp.float32)
                + own_in[rows].astype(jnp.float32)
                + across_in[rows].astype(jnp.float32)
            )

    for kind in range(3):
        for k in range(len(chunks)):
            copy(kind, k).wait_send()
    run_guests(made)


def startup_kernel(nf, nc, spans, row_count, *refs):
    ring_count = len(spans)
    total = ring_count + row_count
    ins, outs, sems, extra = split_refs(refs, (total, total, total, 3))
    block, trade_sems, give_sems = extra
    rest = ins[0].shape[1] * nf - block.shape[0]
    rest = rest // (nf - 1)
    thin = ins[0].shape[1] - rest
    trade = Trade(
        "fsdp",
        nf,
        lambda k: ins[0].at[k, pl.ds(0, thin)],
        lambda k: block.at[pl.ds(pl.multiple_of(k * thin, 8), thin)],
        trade_sems,
    )
    giver = lax.axis_index("ctx") // (nc // nf)
    shard = lax.axis_index("fsdp")

    def give(k):
        return mesh_copy(
            ins[0].at[(shard + k) % nf, pl.ds(thin, rest)],
            block.at[pl.ds(nf * thin, rest)],
            give_sems.at[0, k],
            give_sems.at[1, 0],
            ((shard + k) % nf, lax.axis_index("ctx")),
        )

    own_rest = pltpu.make_async_copy(
        ins[0].at[shard, pl.ds(thin, rest)],
        block.at[pl.ds(nf * thin, rest)],
        give_sems.at[0, 0],
    )
    parts = functools.partial(joint_parts, nf, nc, block.shape[0], outs[0].shape[0])
    rings = [
        RingGather(nc, block if k == 0 else ins[k], outs[k], sems[k], None if k else parts)
        for k in range(ring_count)
    ]
    sides = [FsdpGather(ins[k], outs[k], sems[k]) for k in range(ring_count, total)]
    greet(fsdp_peers(3) + ring_peers(nc))
    trade.begin()

    @pl.when(shard == giver)
    def _():
        own_rest.start()
        for k in range(1, nf):
            give(k).start()

    for ring in rings[1:]:
        ring.start(1)
    sides[0].begin()
    trade.finish()

    @pl.when(shard == giver)
    def _():
        own_rest.wait()
        for k in range(1, nf):
            give(k).wait_send()

    @pl.when(shard != giver)
    def _():
        give(1).wait_recv()

    rings[0].start(1)
    sides[0].pass_on()
    for side in sides[1:]:
        side.begin()
    for step in range(2, nc // 2 + 1):
        for ring, span in zip(rings, spans):
            if step <= span:
                ring.advance(step)
        if step == 2:
            for side in sides[1:]:
                side.pass_on()
    for side in sides:
        side.finish()
    for ring, span in zip(rings, spans):
        ring.finish(1, span)


def in_vmem():
    return pl.BlockSpec(memory_space=pltpu.VMEM)


def in_place():
    return pl.BlockSpec(memory_space=pl.ANY)


def widen(pieces):
    return jnp.pad(pieces, ((0, 0),) * (pieces.ndim - 1) + ((0, -pieces.shape[-1] % LANES),))


class Net:
    def __init__(self, nf, nc):
        self.nf, self.nc = nf, nc
        self.each = nc // nf
        self.ids = {}

    def call(self, kernel, key, outs, ins, in_specs, out_specs, scratch, aliases=None):
        ident = self.ids.setdefault(key, len(self.ids))
        return pl.pallas_call(
            kernel,
            out_shape=outs,
            in_specs=in_specs,
            out_specs=out_specs,
            scratch_shapes=scratch,
            input_output_aliases=aliases or {},
            compiler_params=pltpu.CompilerParams(
                collective_id=ident, has_side_effects=True, vmem_limit_bytes=60 << 20
            ),
        )(*ins)

    def swap(self, blocks, move, back):
        place = lax.axis_index("ctx")
        got = []
        for turn in range(self.each):
            slot = (move(0, place, 0)[2] + turn) % self.each
            piece = lax.dynamic_index_in_dim(blocks, slot, 0, keepdims=False)
            pairs = []
            for f in range(self.nf):
                for c in range(self.nc):
                    there = move(f, c, (move(f, c, 0)[2] + turn) % self.each)
                    pairs.append((f * self.nc + c, there[0] * self.nc + there[1]))
            got.append(lax.ppermute(piece, ("fsdp", "ctx"), pairs))
        order = (back(0, place, 0)[2] - jnp.arange(self.each)) % self.each
        return pick(jnp.stack(got), order)

    def total(self, mine, right, left):
        own = lax.dynamic_index_in_dim(mine, lax.axis_index("ctx"), 0, keepdims=False)
        return sum(part.astype(jnp.float32) for part in (own, right, left)).astype(mine.dtype)

    def lone(self, name, hosted_steps):
        plan, ins, outs, scratch, aliases = self.guests(hosted_steps, 0, 0)
        return self.call(
            functools.partial(lone_kernel, self.nf, self.nc, plan),
            name,
            tuple(outs),
            ins,
            self.specs(hosted_steps),
            [in_place()] * len(outs),
            scratch,
            aliases,
        )

    def specs(self, hosted_steps):
        made = []
        for kind, _, arrays in hosted_steps:
            made += [in_vmem() if kind.VMEM_IN else in_place()] * len(arrays)
        return made

    def startup(self, pieces, block_rows, whole_rows, blocks, spans, rows):
        nf, nc = self.nf, self.nc
        first = (block_rows, pieces.shape[2])
        arrays = [pieces] + list(blocks) + list(rows)
        outs = [jax.ShapeDtypeStruct((whole_rows, pieces.shape[2]), pieces.dtype)]
        outs += [jax.ShapeDtypeStruct((nc,) + a.shape, a.dtype) for a in blocks]
        outs += [jax.ShapeDtypeStruct((nf,) + a.shape, a.dtype) for a in rows]
        scratch = [pltpu.SemaphoreType.DMA((5, nc // 2, nf + 1)) for _ in range(1 + len(blocks))]
        scratch += [pltpu.SemaphoreType.DMA(FsdpGather.SEMS) for _ in rows]
        scratch += [pltpu.VMEM(first, pieces.dtype)] + [pltpu.SemaphoreType.DMA((3, nf))] * 2
        count = len(arrays)
        return self.call(
            functools.partial(startup_kernel, nf, nc, tuple(spans), len(rows)),
            "startup", tuple(outs), arrays, [in_vmem()] * count, [in_place()] * count, scratch,
        )

    def guests(self, hosted_steps, first_in, first_out):
        plan, ins, outs, scratch, aliases = [], [], [], [], {}
        for kind, step, arrays in hosted_steps:
            shapes, boxes, alias = kind.shapes(self.nf, self.nc, step, arrays)
            if alias:
                aliases[first_in + len(ins)] = first_out + len(outs)
            plan.append((kind, step, len(arrays), len(shapes), len(boxes)))
            ins += list(arrays)
            outs += shapes
            scratch += boxes
        return tuple(plan), ins, outs, scratch, aliases

    def gather_fsdp(self, name, rows, hosted_steps=()):
        plan, ins, outs, scratch, aliases = self.guests(hosted_steps, 1, 1)
        got = self.call(
            functools.partial(gather_fsdp_kernel, self.nf, self.nc, plan),
            name,
            (jax.ShapeDtypeStruct((self.nf,) + rows.shape, rows.dtype),) + tuple(outs),
            [rows] + ins,
            [in_vmem()] + self.specs(hosted_steps),
            [in_place()] * (1 + len(outs)),
            [pltpu.SemaphoreType.DMA(FsdpGather.SEMS)] + scratch,
            aliases,
        )
        return got[0].reshape((-1,) + rows.shape[1:]), got[1:]

    def scatter_fsdp(self, name, left, right, turned, hosted_steps=()):
        plan, ins, outs, scratch, aliases = self.guests(hosted_steps, 2, 1)
        count = left.shape[0] // self.nf
        block = (count, right.shape[0] if turned else right.shape[1])
        box = pltpu.VMEM(block, left.dtype)
        got = self.call(
            functools.partial(scatter_fsdp_kernel, self.nf, self.nc, plan, turned),
            name,
            (jax.ShapeDtypeStruct(block, jnp.float32),) + tuple(outs),
            [left, right] + ins,
            [in_vmem(), in_vmem()] + self.specs(hosted_steps),
            [in_vmem()] + [in_place()] * len(outs),
            [pltpu.VMEM((self.nf,) + block, left.dtype), box, box, box, box]
            + [pltpu.SemaphoreType.DMA((6, 4))]
            + scratch,
            aliases,
        )
        return got[0], got[1:]

    def attend_forward(self, segs, qkv, hosted_steps):
        rows, wide = qkv.shape
        slots = wide // 3
        pairs = slots // LANES
        plan, ins, outs, scratch, aliases = self.guests(hosted_steps, 3, 3)
        low = jnp.bfloat16
        got = self.call(
            functools.partial(attend_forward_kernel, self.nf, self.nc, plan),
            "attend_forward",
            (
                jax.ShapeDtypeStruct((rows, slots), low),
                jax.ShapeDtypeStruct((pairs, LANES, rows), jnp.float32),
                jax.ShapeDtypeStruct((pairs, 2, rows), jnp.float32),
            )
            + tuple(outs),
            [segs.reshape(1, rows), segs.reshape(rows, 1), qkv] + ins,
            [in_vmem()] * 3 + self.specs(hosted_steps),
            [in_vmem()] * 3 + [in_place()] * len(outs),
            [
                pltpu.VMEM((rows, LANES), low),
                pltpu.VMEM((rows, LANES), low),
                pltpu.VMEM((rows, LANES), low),
                pltpu.VMEM((LANES, rows), low),
                pltpu.VMEM((LANES, TILE), jnp.float32),
                pltpu.VMEM((2, 1, TILE), jnp.float32),
                pltpu.VMEM((2, 1, TILE), jnp.float32),
            ]
            + scratch,
            aliases,
        )
        return got[:3], got[3:]

    def attend_backward(self, segs, qkv, grads, turned, lse, hosted_steps):
        rows, wide = qkv.shape
        plan, ins, outs, scratch, aliases = self.guests(hosted_steps, 6, 1)
        low = jnp.bfloat16
        got = self.call(
            functools.partial(attend_backward_kernel, self.nf, self.nc, plan),
            "attend_backward",
            (jax.ShapeDtypeStruct((rows, wide), low),) + tuple(outs),
            [segs.reshape(1, rows), segs.reshape(rows, 1), qkv, grads, turned, lse] + ins,
            [in_vmem()] * 6 + self.specs(hosted_steps),
            [in_vmem()] + [in_place()] * len(outs),
            [
                pltpu.VMEM((rows, LANES), low),
                pltpu.VMEM((rows, LANES), low),
                pltpu.VMEM((rows, LANES), low),
                pltpu.VMEM((LANES, rows), low),
                pltpu.VMEM((rows, LANES), low),
                pltpu.VMEM((rows, LANES), low),
                pltpu.VMEM((rows, LANES), low),
                pltpu.VMEM((LANES, TILE), jnp.float32),
                pltpu.VMEM((rows, LANES), jnp.float32),
                pltpu.VMEM((rows, LANES), jnp.float32),
                pltpu.VMEM((2, 1, rows), jnp.float32),
            ]
            + scratch,
            aliases,
        )
        return got[0], got[1:]


def local_fast(
    net,
    inputs,
    cotangent,
    segments,
    stretch_order,
    prenorm_gain,
    prenorm_shift,
    joint_weight,
    query_bias,
    value_bias,
    mixer_weight,
    mixer_bias,
    midnorm_gain,
    midnorm_shift,
    expand_weight,
    expand_bias,
    shrink_weight,
    shrink_bias,
):
    nf, nc, each = net.nf, net.nc, net.each
    low, wide = jnp.bfloat16, jnp.float32
    _, stretch_len, width = inputs.shape
    heads_each = -(-(width // HEAD) // nf)
    span = heads_each * HEAD
    slots = slot_width(heads_each)
    rows_all = nc * stretch_len
    rows_own = each * stretch_len
    shard = lax.axis_index("fsdp")
    positions = stretch_order.reshape(each, nf).T.reshape(nc)
    inverse = jnp.sum(
        jnp.where(
            positions[None, :] == jnp.arange(nc, dtype=jnp.int32)[:, None],
            jnp.arange(nc, dtype=jnp.int32)[None, :],
            0,
        ),
        axis=1,
    ).astype(jnp.int32)

    narrow = prenorm_gain.shape[0]
    unit_each = expand_bias.shape[0] // nf

    depth = joint_weight.shape[0]
    thin = depth // (8 * nc) * 8
    rest = (depth - nc * thin) // each
    out_each = shrink_weight.shape[1]
    small_parts = (
        prenorm_gain, prenorm_shift, query_bias, value_bias, mixer_bias,
        midnorm_gain, midnorm_shift, shrink_bias, expand_bias,
    )
    small_count = len(small_parts) - 1 + nf
    small_rows = small_count + -small_count % 16
    last_rows = ((len(small_parts) - 1, small_rows - small_count), (0, 0))
    small_own = rows_of(small_parts[:-1], small_rows) + jnp.pad(
        expand_bias.reshape(nf, narrow), last_rows
    )
    small_own = widen(small_own)
    step = span - mixer_weight.shape[0]
    most = step * (nf - 1)
    columns = joint_weight.shape[1]
    joint_tall = jnp.concatenate(
        [
            joint_weight[: nc * thin].reshape(nc, thin, columns),
            jnp.tile(joint_weight[nc * thin :].reshape(each, rest, columns), (nf, 1, 1)),
        ],
        axis=1,
    )
    seg_own = jnp.broadcast_to(segments.astype(low)[:, None], (each, 16, stretch_len))
    joint_pieces, small_all, own_tokens, seg_own, above, expand_pieces, shrink_pieces = (
        net.lone(
            "first",
            [
                (TradeGuest, ("ctx", None), [widen(joint_tall)]),
                (TradeGuest, ("ctx", None), [small_own]),
                (SwapGuest, "column", [inputs]),
                (SwapGuest, "column", [seg_own]),
                (TradeGuest, ("fsdp", (nf - 1,)), [widen(mixer_weight[:most])]),
                (
                    TradeGuest,
                    ("fsdp", None),
                    [widen(expand_weight.T.reshape(nf, unit_each, depth))],
                ),
                (
                    TradeGuest,
                    ("fsdp", None),
                    [
                        widen(
                            shrink_weight.reshape(each, nf, unit_each, out_each)
                            .transpose(1, 0, 2, 3)
                            .reshape(nf, each * unit_each, out_each)
                        )
                    ],
                ),
            ],
        )
    )
    own_tokens = own_tokens.reshape(rows_own, width)
    joint_pieces = joint_pieces[..., :columns].transpose(1, 0, 2)
    joint_pieces = joint_split(joint_pieces.reshape(thin + rest, 3, width), nf, heads_each)
    expand_pieces = (
        expand_pieces[..., :depth].transpose(1, 0, 2).reshape(unit_each, width)
    )
    shrink_pieces = shrink_pieces[..., :out_each].reshape(nc * unit_each, out_each).T

    above = lax.dynamic_index_in_dim(above, (shard + 1) % nf, 0, keepdims=False)
    above = above[:, : mixer_weight.shape[1]]
    tall = jnp.concatenate([mixer_weight, above, jnp.zeros_like(above)])
    mixer_rows = lax.dynamic_slice_in_dim(tall, step * shard, span, 0)
    kept = shard * span + jnp.arange(span, dtype=jnp.int32) < width
    mixer_rows = jnp.where(kept[:, None], mixer_rows, jnp.zeros_like(mixer_rows))
    mixer_pieces = jnp.pad(mixer_rows.T, ((0, 0), (0, slots - span)))

    joint, mixer, expand, shrink, tokens, seg_blocks = net.startup(
        joint_pieces,
        nf * thin + rest,
        width,
        [mixer_pieces, expand_pieces, shrink_pieces],
        [nc // 2, nc // 2, 1, 1],
        [own_tokens, seg_own.reshape(each * 16, stretch_len)],
    )
    mixer = mixer.reshape(width, slots)
    tokens = tokens.reshape(rows_all, width)
    cotangent, tokens = lax.optimization_barrier((cotangent, tokens))
    own_tangent = net.swap(cotangent, to_column, to_origin).reshape(rows_own, width)
    segs = pick(seg_blocks.reshape(nc, 16, stretch_len)[:, 0], inverse)
    segs = segs.astype(jnp.int32)
    small_all = small_all[:, :small_count, :narrow].transpose(1, 0, 2).astype(wide)
    gain_one, shift_one, qbias, vbias, mbias, gain_two, shift_two, sbias = (
        small_all[: small_count - nf].reshape(small_count - nf, width)
    )
    ebias = small_all[small_count - nf :].reshape(nf, nc, unit_each)
    ebias = all_units(ebias, nc, nf, unit_each, shard)
    joint_bias = lax.dynamic_index_in_dim(
        joint_split(
            jnp.stack([qbias, jnp.zeros_like(qbias), vbias])[None], nf, heads_each
        ),
        shard, 0, keepdims=False,
    )

    tokens = pick(tokens.reshape(nc, stretch_len, width), inverse)
    token_values = tokens.reshape(rows_all, width).astype(wide)
    unit_one, _ = normalize(token_values)
    normed = (unit_one * gain_one + shift_one).astype(low)
    qkv = (
        jnp.dot(normed, joint, preferred_element_type=wide) + joint_bias
    ).astype(low)
    (attended, turned, lse), (expand, shrink, tangent) = net.attend_forward(
        segs,
        qkv,
        [
            (GatherStep, 2, [expand]),
            (GatherStep, 2, [shrink]),
            (SideGather, 0, [own_tangent]),
        ],
    )
    attended = pick(attended.reshape(nc, stretch_len, slots), positions)
    attended = attended.reshape(rows_all, slots)
    branch, (expand, shrink) = net.scatter_fsdp(
        "scatter_branch",
        attended,
        mixer,
        True,
        [
            (GatherStep, 3, [expand]),
            (GatherStep, 3, [shrink]),
        ],
    )
    tangent = tangent.reshape(rows_all, width)
    middle = own_tokens.astype(wide) + branch + mbias
    unit_two, inverse_two = normalize(middle)
    second_own = (unit_two * gain_two + shift_two).astype(low)
    second, (expand, shrink) = net.gather_fsdp(
        "gather_second", second_own, [(GatherStep, 4, [expand]), (GatherStep, 4, [shrink])]
    )
    expand = expand.reshape(nc * unit_each, width)
    shrink = shrink.reshape(width, nc * unit_each)
    expanded = times_transposed(second, expand) + ebias
    active, slope = gelu_parts(expanded)
    active = active.astype(low)

    shrink_rows = outer_sum(tangent, active).astype(low).reshape(nc, out_each, nc * unit_each)
    active_grad = jnp.dot(tangent, shrink, preferred_element_type=wide)
    expand_delta = (active_grad * slope).astype(low)
    expand_rows = outer_sum(expand_delta, second).astype(low).reshape(nc, unit_each, width)
    second_grad, boxes = net.scatter_fsdp(
        "scatter_second",
        expand_delta,
        expand,
        False,
        [(ScatterStep, 1, [expand_rows]), (ScatterStep, 1, [shrink_rows])],
    )
    middle_delta = own_tangent.astype(wide) + normalize_back(
        second_grad, gain_two, unit_two, inverse_two
    )
    branch_own = middle_delta.astype(low)
    branch_delta, boxes = net.gather_fsdp(
        "gather_branch",
        branch_own,
        [(ScatterStep, 2, [expand_rows, *boxes[:2]]), (ScatterStep, 2, [shrink_rows, *boxes[2:]])],
    )
    lifted, boxes = net.scatter_fsdp(
        "scatter_lifted",
        active,
        shrink,
        True,
        [(ScatterStep, 3, [expand_rows, *boxes[:2]]), (ScatterStep, 3, [shrink_rows, *boxes[2:]])],
    )
    out_rows = (middle + lifted + sbias).astype(low)
    block_output = net.swap(out_rows.reshape(each, stretch_len, width), to_origin, to_column)
    attended_delta = jnp.dot(branch_delta, mixer, preferred_element_type=wide).astype(low)
    mixer_rows = outer_sum(branch_delta, attended).astype(low).reshape(nc, out_each, slots)
    attended_delta = pick(attended_delta.reshape(nc, stretch_len, slots), inverse).reshape(
        rows_all, slots
    )
    joint_delta, boxes = net.attend_backward(
        segs,
        qkv,
        attended_delta,
        turned,
        lse,
        [(ScatterStep, 4, [expand_rows, *boxes[:2]]), (ScatterStep, 4, [shrink_rows, *boxes[2:]])],
    )
    expand_grad = net.total(expand_rows, *boxes[:2])
    shrink_grad = net.total(shrink_rows, *boxes[2:])
    joint_rows = outer_sum(normed, joint_delta).astype(low)
    normed_grad, (joint_grad, mixer_grad, expand_pieces, shrink_pieces) = (
        net.scatter_fsdp(
            "scatter_normed",
            pick(joint_delta.reshape(nc, stretch_len, 3 * slots), positions).reshape(
                rows_all, 3 * slots
            ),
            joint,
            True,
            [
                (ScatterRing, nf * thin + rest, [joint_rows]),
                (ScatterRing, 0, [mixer_rows]),
                (
                    TradeGuest,
                    ("fsdp", None),
                    [widen(expand_grad.reshape(unit_each, nf, depth).transpose(1, 0, 2))],
                ),
                (
                    TradeGuest,
                    ("fsdp", None),
                    [widen(shrink_grad.T.reshape(nf, each * unit_each, out_each))],
                ),
            ],
        )
    )
    unit_own, inverse_own = normalize(own_tokens.astype(wide))
    input_rows = middle_delta + normalize_back(normed_grad, gain_one, unit_own, inverse_own)
    mine = jnp.arange(nf, dtype=jnp.int32) == shard
    sums = jnp.sum(joint_delta.astype(wide), axis=0).reshape(3, slots)[:, :span]
    spread = jnp.where(mine[None, :, None], sums[:, None, :], 0.0).reshape(3, nf * span)
    unit_sums = jnp.sum(expand_delta.astype(wide), axis=0).reshape(nc, 1, unit_each)
    unit_sums = jnp.where(mine[None, :, None], unit_sums, 0.0).reshape(nc, nf * unit_each)
    vectors = (
        jnp.sum(normed_grad * unit_own, axis=0),
        jnp.sum(normed_grad, axis=0),
        spread[0, :width],
        spread[2, :width],
        jnp.sum(branch_own.astype(wide), axis=0),
        jnp.sum(second_grad * unit_two, axis=0),
        jnp.sum(second_grad, axis=0),
        jnp.sum(own_tangent.astype(wide), axis=0),
    )
    stacked = rows_of(vectors, len(vectors)).reshape(len(vectors), nc, narrow)
    unit_sums = unit_sums.reshape(nc, nf, narrow).transpose(1, 0, 2)
    small_blocks = jnp.concatenate(
        [stacked, unit_sums, jnp.zeros((small_rows - small_count, nc, narrow), wide)]
    )
    small_blocks = widen(small_blocks.astype(low)).transpose(1, 0, 2)
    small_lanes = small_blocks.shape[2]

    joint_pieces, joint_last, mixer_pieces, small_pieces, input_gradient = net.lone(
        "second",
        [
            (
                TradeGuest,
                ("fsdp", None),
                [joint_grad[: nf * thin].reshape(nf, thin, 3 * slots)],
            ),
            (TradeGuest, ("fsdp", None), [joint_grad[nf * thin :]]),
            (TradeGuest, ("fsdp", (1,)), [mixer_grad]),
            (TradeGuest, ("fsdp", None), [small_blocks.reshape(nc * small_rows, small_lanes)]),
            (SwapGuest, "origin", [input_rows.astype(low).reshape(each, stretch_len, width)]),
        ],
    )
    input_gradient = input_gradient.astype(wide)
    small_blocks = jnp.sum(small_pieces.astype(wide), axis=0).astype(low)
    joint_pieces = jnp.concatenate([joint_pieces, joint_last], axis=1)
    joint_pieces = joint_join(joint_pieces, heads_each, width)
    joint_pieces = joint_pieces.reshape(thin + rest, nc, columns).transpose(1, 0, 2)
    joint_pieces, small_pieces = net.lone(
        "third",
        [
            (TradeGuest, ("ctx", None), [widen(joint_pieces)]),
            (TradeGuest, ("ctx", None), [small_blocks.reshape(nc, small_rows, small_lanes)]),
        ],
    )
    joint_pieces = joint_pieces[..., :columns]
    joint_last = lax.dynamic_slice_in_dim(joint_pieces[:, thin:], each * shard, each, 0)
    joint_gradient = jnp.concatenate(
        [
            joint_pieces[:, :thin].reshape(nc * thin, columns),
            joint_last.reshape(each * rest, columns),
        ]
    ).astype(wide)
    expand_gradient = expand_pieces[..., :depth].reshape(nf * unit_each, depth).T.astype(wide)
    shrink_pieces = shrink_pieces[..., :out_each].reshape(nf, each, unit_each, out_each)
    shrink_pieces = shrink_pieces.transpose(1, 0, 2, 3)
    shrink_gradient = shrink_pieces.reshape(shrink_weight.shape).astype(wide)

    own_rows = lax.dynamic_index_in_dim(mixer_pieces, shard, 0, keepdims=False)[:, :span].T
    before = lax.dynamic_index_in_dim(mixer_pieces, (shard + nf - 1) % nf, 0, keepdims=False)
    below = lax.dynamic_slice_in_dim(
        jnp.pad(before[:, :span].T, ((0, most), (0, 0))),
        mixer_weight.shape[0] - step * ((shard + nf - 1) % nf),
        most,
        0,
    )
    moved = lax.dynamic_slice_in_dim(
        jnp.pad(own_rows, ((most, 0), (0, 0))), most - step * shard, mixer_weight.shape[0], 0
    )
    first_rows = jnp.arange(mixer_weight.shape[0], dtype=jnp.int32)[:, None] < step * shard
    below = jnp.pad(below, ((0, mixer_weight.shape[0] - most), (0, 0)))
    mixer_gradient = jnp.where(first_rows, below, moved).astype(wide)

    small_sum = jnp.sum(small_pieces.astype(wide), axis=0)[:small_count, :narrow]
    outs = [small_sum[k] for k in range(8)]
    return (
        block_output,
        input_gradient,
        outs[0],
        outs[1],
        joint_gradient,
        outs[2],
        outs[3],
        mixer_gradient,
        outs[4],
        outs[5],
        outs[6],
        expand_gradient,
        small_sum[8:].reshape(expand_bias.shape),
        shrink_gradient,
        outs[7],
    )


def solution(mesh):
    in_specs = (
        P("fsdp", "ctx", None),
        P("fsdp", "ctx", None),
        P("fsdp", "ctx"),
        P(),
        P("ctx"),
        P("ctx"),
        P("fsdp", "ctx"),
        P("ctx"),
        P("ctx"),
        P("fsdp", "ctx"),
        P("ctx"),
        P("ctx"),
        P("ctx"),
        P("fsdp", "ctx"),
        P("ctx"),
        P("fsdp", "ctx"),
        P("ctx"),
    )
    out_specs = (
        P("fsdp", "ctx", None),
        P("fsdp", "ctx", None),
        P("ctx"),
        P("ctx"),
        P("fsdp", "ctx"),
        P("ctx"),
        P("ctx"),
        P("fsdp", "ctx"),
        P("ctx"),
        P("ctx"),
        P("ctx"),
        P("fsdp", "ctx"),
        P("ctx"),
        P("fsdp", "ctx"),
        P("ctx"),
    )

    def run(*arrays):
        nf, nc = mesh.shape["fsdp"], mesh.shape["ctx"]
        whole_each = arrays[0].shape[0] == nc and (nf, nc) == (4, 8)
        if whole_each and arrays[0].shape[1] == nc * STRETCH:
            body = functools.partial(local_fast, Net(nf, nc))
        else:
            body = local
        return jax.shard_map(
            body, mesh=mesh, in_specs=in_specs, out_specs=out_specs, check_vma=False
        )(*arrays)

    return run
```

profile of v0, /device:TPU:0, one launch (start us, length us, event | category | flops | bytes accessed | tf_op | source)
XLA Modules:
  0.0 735.4 jit_solution(6081873078781843965)
XLA Ops:
  9.4 3.8 reshape.627
  17.7 42.6 %shard_map.280 = (bf16[8,56,640]{2,1,0:T(8,128)(2,1)}, bf16[8,16,256]{2,1,0:T(8,128)(2,1)}, bf16[2,128,1600]{2,1,0:T(8,128)(2,1)}, bf16[2,16,128]{2,1,0:T(8,128)...) custom-call(bf16[8,56,640]{2,1,0:T(8,128)(2,1)} %fusion.31.refs_0_, ...), custom_call_target="tpu_custom_call" | custom-call | tf_op jit(solution)/shard_map/pallas_call | solution.py:1837
  66.9 1.7 reshape.632.refs_0_
  70.3 1.6 reshape.633.refs_2_
  71.9 102.2 %shard_map.281 = (bf16[1600,1536]{1,0:T(8,128)(2,1)}, bf16[8,200,512]{2,1,0:T(8,128)(2,1)}, bf16[8,200,1600]{2,1,0:T(8,128)(2,1)}, bf16[8,200,1600]{2,1,0:T(8,12...) custom-call(bf16[4,56,1536]{2,1,0:T(8,128)(2,1)} %reshape.632.refs_0_, ...), custom_call_target="tpu_custom_call" | custom-call | tf_op jit(solution)/shard_map/pallas_call | solution.py:1837
  175.0 4.9 collective-permute-start
  179.9 3.2 collective-permute-start.1
  190.9 3.1 gather_fusion.1
  197.6 2.2 fusion.10
  199.9 10.9 %add_convert_fusion.refs_2_ = bf16[1024,1536]{1,0:T(8,128)(2,1)} fusion(bf16[1024,1600]{1,0:T(8,128)(2,1)S(1)} %fusion.10, bf16[1600,1536]{1,0:T(8,128)(2,1)} %get-tuple-element.84.refs_1_, f32[1536]{0:T(1024)S(1)} %dynamic-slice_reduce_fusion.1), kind=kOutput, calls=%fused_computation.28 | convolution fusion | flops 5036310528 | bytes 11343872 | tf_op jit(solution)/shard_map/dot_general | solution.py:2154
  218.0 35.6 %shard_map.282 = (bf16[1024,512]{1,0:T(8,128)(2,1)}, f32[4,128,1024]{2,1,0:T(8,128)}, f32[4,2,1024]{2,1,0:T(2,128)}, bf16[8,200,1600]{2,1,0:T(8,128)(2,1)}, bf16...) custom-call(s32[1,1024]{1,0:T(1,128)} %bitcast.224, ...), custom_call_target="tpu_custom_call", output_to_operand_aliasing={{3}: (3, {}), {4}: (4, {})} | custom-call | tf_op jit(solution)/shard_map/pallas_call | solution.py:1837
  253.7 2.9 gather_fusion.3
  256.6 35.5 %shard_map.283 = (f32[256,1600]{1,0:T(8,128)}, bf16[8,200,1600]{2,1,0:T(8,128)(2,1)}, bf16[8,200,1600]{2,1,0:T(8,128)(2,1)}) custom-call(bf16[1024,512]{1,0:T(8,128)(2,1)} %bitcast.191, bf16[1600,512]{1,0:T(8,128)(2,1)} %bitcast.206, bf16[8,200,1600]{2,1,0:T(8,128)(2,1)} %get-tuple-element.90.refs_2_, ...), custom_call_target="tpu_custom_call", output_to_operand_aliasing={{1}: (2, {}), {2}: (3, {})} | custom-call | tf_op jit(solution)/shard_map/pallas_call | solution.py:1837
  292.1 1.8 fusion.44
  295.5 23.8 %shard_map.284 = (bf16[4,256,1600]{2,1,0:T(8,128)(2,1)}, bf16[8,200,1600]{2,1,0:T(8,128)(2,1)}, bf16[8,200,1600]{2,1,0:T(8,128)(2,1)}) custom-call(bf16[256,1600]{1,0:T(8,128)(2,1)} %add_convert_fusion.2.refs_0_, bf16[8,200,1600]{2,1,0:T(8,128)(2,1)} %get-tuple-element.93.refs_1_, ...), custom_call_target="tpu_custom_call", output_to_operand_aliasing={{1}: (1, {}), {2}: (2, {})} | custom-call | tf_op jit(solution)/shard_map/pallas_call | solution.py:1837
  319.4 10.9 %multiply_convert_fusion = (bf16[1024,1600]{1,0:T(8,128)(2,1)S(1)}, f32[1024,1600]{1,0:T(8,128)S(1)}) fusion(f32[1600]{0:T(1024)S(1)} %add.329, bf16[1024,1600]{1,0:T(8,128)(2,1)} %bitcast.241, bf16[1600,1600]{1,0:T(8,128)(2,1)} %bitcast.185), kind=kOutput, calls=%fused_computation.25 | convolution fusion | flops 5259264000 | bytes 18233600 | tf_op jit(solution)/shard_map/dot_general | solution.py:46
  330.3 9.2 %convert_reduce_fusion = (bf16[1600]{0:T(1024)(128)(2,1)S(1)}, bf16[1024,1600]{1,0:T(8,128)(2,1)S(1)}) fusion(f32[1024,1600]{1,0:T(8,128)S(1)} %get-tuple-element.220, f32[1600]{0:T(1024)S(1)} %add.329, bf16[1024,1600]{1,0:T(8,128)(2,1)S(1)} %bitcast.239, bf16[1600,1600]{1,0:T(8,128)(2,1)S(1)} %bitcast.184), kind=kOutput, calls=%fused_computation.24 | convolution fusion | flops 5278923264 | bytes 18236800 | tf_op jit(solution)/shard_map/dot_general | solution.py:2191
  339.5 8.7 %convolution_convert_fusion.2 = bf16[1600,1600]{1,0:T(8,128)(2,1)} fusion(bf16[1024,1600]{1,0:T(8,128)(2,1)S(1)} %get-tuple-element.222.refs_0_, bf16[1024,1600]{1,0:T(8,128)(2,1)S(1)} %bitcast.242), kind=kOutput, calls=%fused_computation.11 | convolution fusion | flops 5245440000 | bytes 11673600 | tf_op jit(solution)/shard_map/dot_general | solution.py:52
  348.2 8.7 %convolution_convert_fusion.1 = bf16[1600,1600]{1,0:T(8,128)(2,1)} fusion(bf16[1024,1600]{1,0:T(8,128)(2,1)S(1)} %bitcast.240, bf16[1024,1600]{1,0:T(8,128)(2,1)S(1)} %get-tuple-element.219.refs_0_), kind=kOutput, calls=%fused_computation.10 | convolution fusion | flops 5245440000 | bytes 11673600 | tf_op jit(solution)/shard_map/dot_general | solution.py:52
  356.9 29.0 %shard_map.285 = (f32[256,1600]{1,0:T(8,128)}, bf16[200,1600]{1,0:T(8,128)(2,1)}, bf16[200,1600]{1,0:T(8,128)(2,1)}, bf16[200,1600]{1,0:T(8,128)(2,1)}, bf16[200,1600]{1,0:T(8,128)(2,1)}) custom-call(bf16[1024,1600]{1,0:T(8,128)(2,1)} %copy-done.11, bf16[1600,1600]{1,0:T(8,128)(2,1)} %bitcast.186, bf16[8,200,1600]{2,1,0:T(8,128)(2,1)} %bitcast.178, ...), custom_call_target="tpu_custom_call" | custom-call | tf_op jit(solution)/shard_map/pallas_call | solution.py:1837
  385.9 2.3 multiply_reduce_fusion.1
  388.3 2.3 convert_reduce_fusion.4
  390.6 35.2 %shard_map.286 = (bf16[4,256,1600]{2,1,0:T(8,128)(2,1)}, bf16[200,1600]{1,0:T(8,128)(2,1)}, bf16[200,1600]{1,0:T(8,128)(2,1)}, bf16[200,1600]{1,0:T(8,128)(2,1)}, bf16[200,1600]{1,0:T(8,128)(2,1)}) custom-call(bf16[256,1600]{1,0:T(8,128)(2,1)} %get-tuple-element.197.refs_0_, bf16[8,200,1600]{2,1,0:T(8,128)(2,1)} %bitcast.179, ...), custom_call_target="tpu_custom_call" | custom-call | tf_op jit(solution)/shard_map/pallas_call | solution.py:1837
  425.8 5.6 convolution_convert_fusion.4
  431.5 3.1 convolution_convert_fusion.3
  434.5 2.9 gather_fusion.5
  437.5 38.8 %shard_map.287 = (f32[256,1600]{1,0:T(8,128)}, bf16[200,1600]{1,0:T(8,128)(2,1)}, bf16[200,1600]{1,0:T(8,128)(2,1)}, bf16[200,1600]{1,0:T(8,128)(2,1)}, bf16[200,1600]{1,0:T(8,128)(2,1)}) custom-call(bf16[1024,1600]{1,0:T(8,128)(2,1)} %copy-done.10, bf16[1600,1600]{1,0:T(8,128)(2,1)} %bitcast.183, bf16[8,200,1600]{2,1,0:T(8,128)(2,1)} %bitcast.180, ...), custom_call_target="tpu_custom_call" | custom-call | tf_op jit(solution)/shard_map/pallas_call | solution.py:1837
  476.3 38.1 %shard_map.288 = (bf16[1024,1536]{1,0:T(8,128)(2,1)}, bf16[200,1600]{1,0:T(8,128)(2,1)}, bf16[200,1600]{1,0:T(8,128)(2,1)}, bf16[200,1600]{1,0:T(8,128)(2,1)}, bf16[200,1600]{1,0:T(8,128)(2,1)}) custom-call(s32[1,1024]{1,0:T(1,128)} %bitcast.225, s32[1024,1]{1,0:T(8,128)} %copy.96.refs_1_, bf16[1024,1536]{1,0:T(8,128)(2,1)} %add_convert_fusion.refs_2_, ...), custom_call_target="tpu_custom_call" | custom-call | tf_op jit(solution)/shard_map/pallas_call | solution.py:1837
  514.4 2.4 convert_reduce_fusion.1
  516.8 9.7 %convolution_convert_fusion.refs_2_ = bf16[1600,1536]{1,0:T(8,128)(2,1)} fusion(bf16[1024,1600]{1,0:T(8,128)(2,1)} %copy-done.9, bf16[1024,1536]{1,0:T(8,128)(2,1)} %get-tuple-element.116), kind=kOutput, calls=%fused_computation.9 | convolution fusion | flops 5035622400 | bytes 11337728 | tf_op jit(solution)/shard_map/dot_general | solution.py:52
  526.5 2.2 fusion.27
  528.8 3.2 reshape.660
  533.5 2.2 fusion.30
  538.1 4.4 gather_fusion.6
  542.5 74.2 %shard_map.289 = (f32[256,1600]{1,0:T(8,128)}, bf16[200,1536]{1,0:T(8,128)(2,1)}, bf16[200,512]{1,0:T(8,128)(2,1)}, bf16[4,200,512]{2,1,0:T(8,128)(2,1)}, bf16[4,400,256]{2,1,0:T(8,128)(2,1)}) custom-call(bf16[1024,1536]{1,0:T(8,128)(2,1)} %bitcast.189, bf16[1600,1536]{1,0:T(8,128)(2,1)} %get-tuple-element.84.refs_1_, ...), custom_call_target="tpu_custom_call" | custom-call | tf_op jit(solution)/shard_map/pallas_call | solution.py:1837
  618.2 1.9 slice.136
  620.6 1.6 add_convert_fusion.1
  626.2 4.9 collective-permute-start.2
  634.5 1.6 fusion.21
  636.1 29.8 %shard_map.290 = (bf16[4,48,1536]{2,1,0:T(8,128)(2,1)}, bf16[4,8,1536]{2,1,0:T(8,128)(2,1)}, bf16[4,200,512]{2,1,0:T(8,128)(2,1)}, bf16[4,128,256]{2,1,0:T(8,128)(2,1)}, bf16[2,128,1600]{2,1,0:T(8,128)(2,1)}) custom-call(bf16[4,48,1536]{2,1,0:T(8,128)(2,1)} %bitcast.202, bf16[8,1536]{1,0:T(8,128)(2,1)} %slice.137.refs_1_, ...), custom_call_target="tpu_custom_call" | custom-call | tf_op jit(solution)/shard_map/pallas_call | solution.py:1837
  665.9 1.6 reduce_sum.214
  675.2 39.2 %shard_map.291 = (bf16[8,56,640]{2,1,0:T(8,128)(2,1)}, bf16[8,16,256]{2,1,0:T(8,128)(2,1)}) custom-call(bf16[8,56,640]{2,1,0:T(8,128)(2,1)} %pad.83.refs_0_, bf16[8,16,256]{2,1,0:T(8,128)(2,1)} %bitcast.220), custom_call_target="tpu_custom_call" | custom-call | tf_op jit(solution)/shard_map/pallas_call | solution.py:1837
  719.4 1.6 copy.108
  721.0 1.9 copy.111
  723.6 2.4 copy.110
  726.8 2.8 reshape.677
  729.7 2.1 maximum_convert_fusion
  733.5 1.7 gather_fusion.4
  (252 shorter events, 71.2 us)
Async XLA Ops:
  8.4 6.6 copy-start.12
  9.4 6.8 slice-start
  65.1 3.5 copy-start.15
  66.0 3.8 copy-start.14
  69.8 104.3 %copy-start.17 = (bf16[2,128,1600]{1,2,0:T(8,128)(2,1)S(1)}, bf16[2,128,1600]{1,2,0:T(8,128)(2,1)}, u32[]{:S(2)}) copy-start(bf16[2,128,1600]{1,2,0:T(8,128)(2,1)} %param.18) | copy-start | bytes 2457604
  70.3 113.4 %copy-start.43 = (s32[8]{0:T(128)S(1)}, s32[8]{0:T(128)}, u32[]{:S(2)}) copy-start(s32[8]{0:T(128)} %param.20) | copy-start | bytes 100
  70.3 115.9 %copy-start.1 = (bf16[2,128,1600]{2,1,0:T(8,128)(2,1)S(1)}, bf16[2,128,1600]{2,1,0:T(8,128)(2,1)}, u32[]{:S(2)}) copy-start(bf16[2,128,1600]{2,1,0:T(8,128)(2,1)} %get-tuple-element.74) | copy-start | bytes 2457604
  70.3 118.6 %copy-start.24 = (bf16[8,16,256]{2,1,0:T(8,128)(2,1)S(1)}, bf16[8,16,256]{2,1,0:T(8,128)(2,1)}, u32[]{:S(2)}) copy-start(bf16[8,16,256]{2,1,0:T(8,128)(2,1)} %get-tuple-element.83) | copy-start | bytes 196612
  175.0 39.4 %collective-permute-start = (bf16[128,1600]{0,1:T(8,128)(2,1)}, bf16[128,1600]{0,1:T(8,128)(2,1)}, u32[]{:S(2)}, u32[]{:S(2)}) collective-permute-start(bf16[128,1600]{0,1:T(8,128)(2,1)} %get-tuple-element.205), channel_id=1, source_target_pairs={{0,0},{1,8},{2,16},{3,24},{4,4},{5,12},{6,20},{7,28},{8,3},{9,11},... | collective-permute-start | bytes 1228808 | tf_op jit(solution)/shard_map/ppermute | solution.py:1860
  179.9 34.5 %collective-permute-start.1 = (bf16[128,1600]{0,1:T(8,128)(2,1)}, bf16[128,1600]{0,1:T(8,128)(2,1)}, u32[]{:S(2)}, u32[]{:S(2)}) collective-permute-start(bf16[128,1600]{0,1:T(8,128)(2,1)} %get-tuple-element.206), channel_id=1, source_target_pairs={{0,4},{1,12},{2,20},{3,28},{4,0},{5,8},{6,16},{7,24},{8,7},{9,15},... | collective-permute-start | bytes 1228808 | tf_op jit(solution)/shard_map/ppermute | solution.py:1860
  199.8 10.9 %copy-start.9 = (bf16[1024,1600]{1,0:T(8,128)(2,1)}, bf16[1024,1600]{1,0:T(8,128)(2,1)S(1)}, u32[]{:S(2)}) copy-start(bf16[1024,1600]{1,0:T(8,128)(2,1)S(1)} %fusion.10) | copy-start | bytes 9830404
  199.8 11.0 %copy-start.31 = (pred[4]{0:T(512)(128)(4,1)S(1)}, pred[4]{0:T(512)(128)(4,1)}, u32[]{:S(2)}) copy-start(pred[4]{0:T(512)(128)(4,1)} %iota_compare_fusion.6) | copy-start | bytes 16
  199.8 11.3 %copy-start.28 = (f32[8,200]{1,0:T(8,128)S(1)}, f32[8,200]{1,0:T(8,128)}, u32[]{:S(2)}) copy-start(f32[8,200]{1,0:T(8,128)} %get-tuple-element.186) | copy-start | bytes 19204
  199.8 11.3 %copy-start.27 = (f32[8,200]{1,0:T(8,128)S(1)}, f32[8,200]{1,0:T(8,128)}, u32[]{:S(2)}) copy-start(f32[8,200]{1,0:T(8,128)} %get-tuple-element.188) | copy-start | bytes 19204
  199.9 11.4 %copy-start.26 = (f32[8,200]{1,0:T(8,128)S(1)}, f32[8,200]{1,0:T(8,128)}, u32[]{:S(2)}) copy-start(f32[8,200]{1,0:T(8,128)} %get-tuple-element.187) | copy-start | bytes 19204
  199.9 11.5 %copy-start.25 = (f32[8,200]{1,0:T(8,128)S(1)}, f32[8,200]{1,0:T(8,128)}, u32[]{:S(2)}) copy-start(f32[8,200]{1,0:T(8,128)} %get-tuple-element.189) | copy-start | bytes 19204
  199.9 14.1 %copy-start.2 = (bf16[2,128,1600]{2,1,0:T(8,128)(2,1)S(1)}, bf16[2,128,1600]{2,1,0:T(8,128)(2,1)}, u32[]{:S(2)}) copy-start(bf16[2,128,1600]{2,1,0:T(8,128)(2,1)} %get-tuple-element.74) | copy-start | bytes 2457604
  199.9 14.1 %copy-start.30 = (f32[2,128]{1,0:T(2,128)S(1)}, f32[2,128]{1,0:T(2,128)}, u32[]{:S(2)}) copy-start(f32[2,128]{1,0:T(2,128)} %get-tuple-element.218) | copy-start | bytes 3076
  212.9 5.1 copy-start.23
  319.3 10.9 %copy-start = (bf16[8,200,1600]{2,1,0:T(8,128)(2,1)S(1)}, bf16[8,200,1600]{2,1,0:T(8,128)(2,1)}, u32[]{:S(2)}) copy-start(bf16[8,200,1600]{2,1,0:T(8,128)(2,1)} %get-tuple-element.97) | copy-start | bytes 15360004
  319.4 10.9 %copy-start.40 = (bf16[4,256,1600]{2,1,0:T(8,128)(2,1)S(1)}, bf16[4,256,1600]{2,1,0:T(8,128)(2,1)}, u32[]{:S(2)}) copy-start(bf16[4,256,1600]{2,1,0:T(8,128)(2,1)} %get-tuple-element.98) | copy-start | bytes 9830404
  330.2 18.0 %copy-start.10 = (bf16[1024,1600]{1,0:T(8,128)(2,1)}, bf16[1024,1600]{1,0:T(8,128)(2,1)S(1)}, u32[]{:S(2)}) copy-start(bf16[1024,1600]{1,0:T(8,128)(2,1)S(1)} %get-tuple-element.219.refs_0_) | copy-start | bytes 9830404
  330.3 9.2 %copy-start.41 = (bf16[4,256,1600]{2,1,0:T(8,128)(2,1)S(1)}, bf16[4,256,1600]{2,1,0:T(8,128)(2,1)}, u32[]{:S(2)}) copy-start(bf16[4,256,1600]{2,1,0:T(8,128)(2,1)} %get-tuple-element.95) | copy-start | bytes 9830404
  339.5 8.7 %copy-start.11 = (bf16[1024,1600]{1,0:T(8,128)(2,1)}, bf16[1024,1600]{1,0:T(8,128)(2,1)S(1)}, u32[]{:S(2)}) copy-start(bf16[1024,1600]{1,0:T(8,128)(2,1)S(1)} %get-tuple-element.222.refs_0_) | copy-start | bytes 9830404
  385.9 2.4 copy-start.3
  385.9 2.4 copy-start.6
  425.8 5.7 copy-start.8
  425.8 5.6 copy-start.42
  516.8 9.8 %copy-start.20 = (bf16[200,1600]{1,0:T(8,128)(2,1)S(1)}, bf16[200,1600]{1,0:T(8,128)(2,1)}, u32[]{:S(2)}) copy-start(bf16[200,1600]{1,0:T(8,128)(2,1)} %get-tuple-element.117) | copy-start | bytes 1920004
  516.8 9.8 %copy-start.21 = (bf16[200,1600]{1,0:T(8,128)(2,1)S(1)}, bf16[200,1600]{1,0:T(8,128)(2,1)}, u32[]{:S(2)}) copy-start(bf16[200,1600]{1,0:T(8,128)(2,1)} %get-tuple-element.118) | copy-start | bytes 1920004
  531.9 1.5 copy-start.19
  620.6 10.5 %copy-start.29 = (f32[256]{0:T(256)S(1)}, f32[256]{0:T(256)}, u32[]{:S(2)}) copy-start(f32[256]{0:T(256)} %get-tuple-element.217) | copy-start | bytes 3076
  622.3 8.9 %copy-start.4 = (f32[256,1600]{1,0:T(8,128)S(1)}, f32[256,1600]{1,0:T(8,128)}, u32[]{:S(2)}) copy-start(f32[256,1600]{1,0:T(8,128)} %get-tuple-element.123) | copy-start | bytes 4915204
  622.3 9.9 %copy-start.32 = (pred[8]{0:T(512)(128)(4,1)S(1)}, pred[8]{0:T(512)(128)(4,1)}, u32[]{:S(2)}) copy-start(pred[8]{0:T(512)(128)(4,1)} %get-tuple-element.239) | copy-start | bytes 28
  622.3 9.9 %copy-start.33 = (pred[8]{0:T(512)(128)(4,1)S(1)}, pred[8]{0:T(512)(128)(4,1)}, u32[]{:S(2)}) copy-start(pred[8]{0:T(512)(128)(4,1)} %get-tuple-element.240) | copy-start | bytes 28
  622.3 9.9 %copy-start.34 = (pred[8]{0:T(512)(128)(4,1)S(1)}, pred[8]{0:T(512)(128)(4,1)}, u32[]{:S(2)}) copy-start(pred[8]{0:T(512)(128)(4,1)} %get-tuple-element.237) | copy-start | bytes 28
  622.3 9.9 %copy-start.35 = (pred[8]{0:T(512)(128)(4,1)S(1)}, pred[8]{0:T(512)(128)(4,1)}, u32[]{:S(2)}) copy-start(pred[8]{0:T(512)(128)(4,1)} %get-tuple-element.238) | copy-start | bytes 28
  622.3 9.9 %copy-start.36 = (pred[8]{0:T(512)(128)(4,1)S(1)}, pred[8]{0:T(512)(128)(4,1)}, u32[]{:S(2)}) copy-start(pred[8]{0:T(512)(128)(4,1)} %get-tuple-element.235) | copy-start | bytes 28
  622.3 9.9 %copy-start.37 = (pred[8]{0:T(512)(128)(4,1)S(1)}, pred[8]{0:T(512)(128)(4,1)}, u32[]{:S(2)}) copy-start(pred[8]{0:T(512)(128)(4,1)} %get-tuple-element.236) | copy-start | bytes 28
  622.3 9.9 %copy-start.38 = (pred[8]{0:T(512)(128)(4,1)S(1)}, pred[8]{0:T(512)(128)(4,1)}, u32[]{:S(2)}) copy-start(pred[8]{0:T(512)(128)(4,1)} %get-tuple-element.233) | copy-start | bytes 28
  622.4 9.9 %copy-start.39 = (pred[8]{0:T(512)(128)(4,1)S(1)}, pred[8]{0:T(512)(128)(4,1)}, u32[]{:S(2)}) copy-start(pred[8]{0:T(512)(128)(4,1)} %get-tuple-element.234) | copy-start | bytes 28
  624.7 8.3 %copy-start.13 = (bf16[4,200,512]{2,1,0:T(8,128)(2,1)S(1)}, bf16[4,200,512]{2,1,0:T(8,128)(2,1)}, u32[]{:S(2)}) copy-start(bf16[4,200,512]{2,1,0:T(8,128)(2,1)} %get-tuple-element.131) | copy-start | bytes 2457604
  624.7 107.6 %collective-permute-start.3 = (bf16[128,1600]{0,1:T(8,128)(2,1)}, bf16[128,1600]{0,1:T(8,128)(2,1)}, u32[]{:S(2)}, u32[]{:S(2)}) collective-permute-start(bf16[128,1600]{0,1:T(8,128)(2,1)} %bitcast.218), channel_id=1, source_target_pairs={{0,4},{1,20},{2,28},{3,12},{4,0},{5,16},{6,24},{7,8},{8,5},{9,21},... | collective-permute-start | bytes 1228808 | tf_op jit(solution)/shard_map/ppermute | solution.py:1860
  626.2 106.1 %collective-permute-start.2 = (bf16[128,1600]{0,1:T(8,128)(2,1)}, bf16[128,1600]{0,1:T(8,128)(2,1)}, u32[]{:S(2)}, u32[]{:S(2)}) collective-permute-start(bf16[128,1600]{0,1:T(8,128)(2,1)} %bitcast.217), channel_id=1, source_target_pairs={{0,0},{1,16},{2,24},{3,8},{4,4},{5,20},{6,28},{7,12},{8,1},{9,17},... | collective-permute-start | bytes 1228808 | tf_op jit(solution)/shard_map/ppermute | solution.py:1860
  632.1 2.4 copy-start.5
  674.2 43.3 %copy-start.16 = (bf16[448,200]{0,1:T(8,128)(2,1)S(1)}, bf16[448,200]{0,1:T(8,128)(2,1)}, u32[]{:S(2)}) copy-start(bf16[448,200]{0,1:T(8,128)(2,1)} %slice_bitcast_fusion.4) | copy-start | bytes 537604
  674.3 45.1 %copy-start.7 = (f32[800,400]{1,0:T(8,128)S(1)}, f32[800,400]{1,0:T(8,128)}, u32[]{:S(2)}) copy-start(f32[800,400]{1,0:T(8,128)} %bitcast_convert_fusion) | copy-start | bytes 3840004
  714.4 4.2 copy-start.22
  (1 other events, 1.2 us)
where the time goes:
time: 746 us; the launch traced here: 735 us
  Pallas kernels  524 us (70%)
  local copies, waits for them, and re-layouts  83.3 us (11%)
  matrix products  66.7 us (9%)
  other arithmetic  44.8 us (6%)
  starting transfers between devices  14.4 us (2%)
    pallas_call x12, Pallas kernels, call(): pl.pallas_call(kernel, out_shape=outs, in_specs=in_specs, out_specs=out_s...  524 us
    dot_general x4, matrix products, outer_sum(): lax.dot_general(left, right, (((0,), (0,)), ((), ())), preferred_element_...  30.2 us
    gather x8, local copies, waits for them, and re-layouts, pick(): return blocks.at[order].get(mode='promise_in_bounds', unique_indices=True)  17.8 us
  transfers between devices with their start and end apart: 4, of which 0 were waited for; matrix products, arithmetic and copies ran while one was open for 9% of the time, Pallas kernels for 9%

commit v1 on v0

--- a/solution.py
+++ b/solution.py
@@ -623,7 +623,7 @@
     return same
 
 
-def attend_forward_kernel(nf, nc, guests, *refs):
+def attend_forward_kernel(nf, nc, heads, guests, *refs):
     n_in = sum(g[2] for g in guests)
     n_out = sum(g[3] for g in guests)
     own, ins, results, outs, own_scratch, scratch = split_refs(
@@ -640,11 +640,11 @@
     scale = HEAD ** (-0.5)
     halves = (q_low, q_high)
 
-    def one_block(q_block, k_block, first):
+    def one_block(q_block, k_block, first, count):
         q_at = pl.ds(pl.multiple_of(q_block * TILE, TILE), TILE)
         k_at = pl.ds(pl.multiple_of(k_block * TILE, TILE), TILE)
         same = causal(first, seg_col[k_at, :] == seg_row[:, q_at])
-        for half in range(2):
+        for half in range(count):
             dims = pl.ds(half * HEAD, HEAD)
             scores = times_transposed(keys[k_at, :], halves[half][q_at, :])
             scores = jnp.where(same, scores, masked_score)
@@ -667,8 +667,7 @@
             sums[half] = total
             acc[dims, :] = part
 
-    @pl.loop(0, slots // LANES)
-    def _(pair):
+    def one_pair(pair, count):
         column = pl.multiple_of(pair * LANES, LANES)
         queries = qkv_ref[:, pl.ds(column, LANES)] * jnp.bfloat16(scale)
         low_half = lax.broadcasted_iota(jnp.int32, queries.shape, 1) < HEAD
@@ -680,34 +679,43 @@
 
         @pl.loop(0, qkv_ref.shape[0] // TILE)
         def _(q_block):
-            one_block(q_block, q_block, True)
+            one_block(q_block, q_block, True, count)
 
             @pl.loop(0, q_block)
             def _(k_block):
-                one_block(q_block, k_block, False)
+                one_block(q_block, k_block, False, count)
 
             q_at = pl.ds(pl.multiple_of(q_block * TILE, TILE), TILE)
-            for half in range(2):
+            if count == 1:
+                acc[HEAD:, :] = jnp.zeros((LANES - HEAD, TILE), jnp.float32)
+                lse_ref[pair, pl.ds(1, 1), q_at] = jnp.zeros((1, TILE), jnp.float32)
+            for half in range(count):
                 dims = pl.ds(half * HEAD, HEAD)
                 acc[dims, :] = acc[dims, :] / sums[half]
                 lse_ref[pair, pl.ds(half, 1), q_at] = tops[half] + jnp.log(sums[half])
             turned_ref[pair, :, q_at] = acc[...]
             out_ref[q_at, pl.ds(column, LANES)] = acc[...].T.astype(jnp.bfloat16)
 
+    @pl.loop(0, heads // 2)
+    def _(pair):
+        one_pair(pair, 2)
+
         @pl.when(pair == 2)
         def _():
             pass_on_guests(made)
 
+    if heads % 2:
+        one_pair(heads // 2, 1)
     run_guests(made)
 
 
-def attend_backward_kernel(nf, nc, guests, *refs):
+def attend_backward_kernel(nf, nc, heads, guests, *refs):
     n_in = sum(g[2] for g in guests)
     n_out = sum(g[3] for g in guests)
     own, ins, results, outs, own_scratch, scratch = split_refs(
-        refs, (6, n_in, 1, n_out, 11, len(refs) - n_in - n_out - 18)
-    )
-    seg_row, seg_col, qkv_ref, grad_ref, turned_ref, lse_ref = own
+        refs, (7, n_in, 1, n_out, 11, len(refs) - n_in - n_out - 19)
+    )
+    seg_row, seg_col, qkv_ref, grad_ref, turned_ref, lse_ref, order_ref = own
     out_ref = results[0]
     (
         q_low, q_high, keys, keys_turned, values, g_low, g_high,
@@ -716,18 +724,18 @@
     made = hosted(nf, nc, guests, ins, outs, scratch)
     greet_all(nc, {needs_of(g) for g in guests})
     begin_guests(made)
-    slots = grad_ref.shape[1]
+    slots = grad_ref.shape[2]
     scale = HEAD ** (-0.5)
     q_halves = (q_low, q_high)
     g_halves = (g_low, g_high)
 
-    def one_block(pair, q_block, k_block, first):
+    def one_block(pair, q_block, k_block, first, count):
         q_at = pl.ds(pl.multiple_of(q_block * TILE, TILE), TILE)
         k_at = pl.ds(pl.multiple_of(k_block * TILE, TILE), TILE)
         same = causal(first, seg_col[k_at, :] == seg_row[:, q_at])
         value_sum = value_acc[k_at, :]
         key_sum = key_acc[k_at, :]
-        for half in range(2):
+        for half in range(count):
             dims = pl.ds(half * HEAD, HEAD)
             query_rows = q_halves[half][q_at, :]
             grad_rows = g_halves[half][q_at, :]
@@ -748,15 +756,16 @@
         value_acc[k_at, :] = value_sum
         key_acc[k_at, :] = key_sum
 
-    @pl.loop(0, slots // LANES)
-    def _(pair):
+    def one_pair(pair, count):
         column = pl.multiple_of(pair * LANES, LANES)
         queries = qkv_ref[:, pl.ds(column, LANES)] * jnp.bfloat16(scale)
         low_half = lax.broadcasted_iota(jnp.int32, queries.shape, 1) < HEAD
         zeros = jnp.zeros_like(queries)
         q_low[...] = jnp.where(low_half, queries, zeros)
         q_high[...] = jnp.where(low_half, zeros, queries)
-        grads = grad_ref[:, pl.ds(column, LANES)]
+        grads = jnp.concatenate(
+            [grad_ref[order_ref[k], :, pl.ds(column, LANES)] for k in range(grad_ref.shape[0])]
+        )
         g_low[...] = jnp.where(low_half, grads, zeros)
         g_high[...] = jnp.where(low_half, zeros, grads)
         product = grads.astype(jnp.float32).T * turned_ref[pair]
@@ -768,25 +777,33 @@
         values[...] = qkv_ref[:, pl.ds(2 * slots + column, LANES)]
         key_acc[...] = jnp.zeros_like(key_acc)
         value_acc[...] = jnp.zeros_like(value_acc)
+        if count == 1:
+            query_acc[HEAD:, :] = jnp.zeros((LANES - HEAD, TILE), jnp.float32)
 
         @pl.loop(0, qkv_ref.shape[0] // TILE)
         def _(q_block):
-            one_block(pair, q_block, q_block, True)
+            one_block(pair, q_block, q_block, True, count)
 
             @pl.loop(0, q_block)
             def _(k_block):
-                one_block(pair, q_block, k_block, False)
+                one_block(pair, q_block, k_block, False, count)
 
             q_at = pl.ds(pl.multiple_of(q_block * TILE, TILE), TILE)
             out_ref[q_at, pl.ds(column, LANES)] = (query_acc[...].T * scale).astype(jnp.bfloat16)
 
         out_ref[:, pl.ds(slots + column, LANES)] = key_acc[...].astype(jnp.bfloat16)
         out_ref[:, pl.ds(2 * slots + column, LANES)] = value_acc[...].astype(jnp.bfloat16)
+
+    @pl.loop(0, heads // 2)
+    def _(pair):
+        one_pair(pair, 2)
 
         @pl.when(pair == 0)
         def _():
             send_guests(made)
 
+    if heads % 2:
+        one_pair(heads // 2, 1)
     run_guests(made)
 
 
@@ -1461,6 +1478,44 @@
         self.trade.finish()
 
 
+def window(part, parts, width):
+    size = max(
+        -(-(k + 1) * (width // parts) // LANES) * LANES - k * (width // parts) // LANES * LANES
+        for k in range(parts)
+    )
+    return part * (width // parts) // LANES * LANES, size
+
+
+class WindowTrade:
+    VMEM_IN = 1
+
+    def __init__(self, nf, nc, step, ins, outs, scratch):
+        def source(k):
+            start, size = window(k, nf, step)
+            return ins[0].at[:, pl.ds(pl.multiple_of(start, LANES), size)]
+
+        self.trade = Trade("fsdp", nf, source, lambda k: outs[0].at[k], scratch[0])
+
+    @staticmethod
+    def shapes(nf, nc, step, arrays):
+        (array,) = arrays
+        shape = (nf, array.shape[0], window(0, nf, step)[1])
+        return (
+            [jax.ShapeDtypeStruct(shape, array.dtype)],
+            [pltpu.SemaphoreType.DMA((3, nf))],
+            False,
+        )
+
+    def begin(self):
+        pass
+
+    def send(self):
+        self.trade.begin()
+
+    def finish(self):
+        self.trade.finish()
+
+
 class SwapGuest:
     VMEM_IN = 1
 
@@ -1558,6 +1613,8 @@
     kind, step = guest[0], guest[1]
     if kind is TradeGuest:
         return step[0]
+    if kind is WindowTrade:
+        return "fsdp"
     if kind is SwapGuest:
         return step
     return kind.NEEDS
@@ -1618,13 +1675,14 @@
     run_guests(made)
 
 
-def scatter_fsdp_kernel(nf, nc, guests, turned, *refs):
+def scatter_fsdp_kernel(nf, nc, guests, turned, ordered, *refs):
     n_in = sum(g[2] for g in guests)
     n_out = sum(g[3] for g in guests)
+    count_own = 3 if ordered else 2
     operands, ins, result, outs, own_scratch, scratch = split_refs(
-        refs, (2, n_in, 1, n_out, 6, len(refs) - n_in - n_out - 9)
-    )
-    left_ref, right_ref = operands
+        refs, (count_own, n_in, 1, n_out, 6, len(refs) - n_in - n_out - 7 - count_own)
+    )
+    left_ref, right_ref = operands[:2]
     out_ref = result[0]
     part_ref, first_in, own_in, chip_sum, across_in, sems = own_scratch
     shard, partner, cross, corner = fsdp_places()
@@ -1678,7 +1736,10 @@
         base = partner * (1 - of_two) + shard * of_two
         block = (base + 2 * (1 - pair)) % 4
         start = pl.multiple_of(upper * half, half)
-        rows = left_ref[pl.ds(pl.multiple_of(block * count + start, half), half), :]
+        if ordered:
+            rows = left_ref[operands[2][block * 2 + upper]]
+        else:
+            rows = left_ref[block * 2 + upper]
         for at in range(0, width, 512):
             size = 512 if at + 1024 <= width else width - at
             if turned:
@@ -1818,6 +1879,10 @@
     return pl.BlockSpec(memory_space=pltpu.VMEM)
 
 
+def in_smem():
+    return pl.BlockSpec(memory_space=pltpu.SMEM)
+
+
 def in_place():
     return pl.BlockSpec(memory_space=pl.ANY)
 
@@ -1926,17 +1991,21 @@
         )
         return got[0].reshape((-1,) + rows.shape[1:]), got[1:]
 
-    def scatter_fsdp(self, name, left, right, turned, hosted_steps=()):
-        plan, ins, outs, scratch, aliases = self.guests(hosted_steps, 2, 1)
+    def scatter_fsdp(self, name, left, right, turned, hosted_steps=(), order=None):
         count = left.shape[0] // self.nf
+        own = [left.reshape(2 * self.nf, count // 2, left.shape[1]), right]
+        own += [] if order is None else [order]
+        plan, ins, outs, scratch, aliases = self.guests(hosted_steps, len(own), 1)
         block = (count, right.shape[0] if turned else right.shape[1])
         box = pltpu.VMEM(block, left.dtype)
         got = self.call(
-            functools.partial(scatter_fsdp_kernel, self.nf, self.nc, plan, turned),
+            functools.partial(
+                scatter_fsdp_kernel, self.nf, self.nc, plan, turned, order is not None
+            ),
             name,
             (jax.ShapeDtypeStruct(block, jnp.float32),) + tuple(outs),
-            [left, right] + ins,
-            [in_vmem(), in_vmem()] + self.specs(hosted_steps),
+            own + ins,
+            [in_vmem(), in_vmem(), in_smem()][: len(own)] + self.specs(hosted_steps),
             [in_vmem()] + [in_place()] * len(outs),
             [pltpu.VMEM((self.nf,) + block, left.dtype), box, box, box, box]
             + [pltpu.SemaphoreType.DMA((6, 4))]
@@ -1945,14 +2014,14 @@
         )
         return got[0], got[1:]
 
-    def attend_forward(self, segs, qkv, hosted_steps):
+    def attend_forward(self, segs, qkv, heads, hosted_steps):
         rows, wide = qkv.shape
         slots = wide // 3
         pairs = slots // LANES
         plan, ins, outs, scratch, aliases = self.guests(hosted_steps, 3, 3)
         low = jnp.bfloat16
         got = self.call(
-            functools.partial(attend_forward_kernel, self.nf, self.nc, plan),
+            functools.partial(attend_forward_kernel, self.nf, self.nc, heads, plan),
             "attend_forward",
             (
                 jax.ShapeDtypeStruct((rows, slots), low),
@@ -1977,16 +2046,16 @@
         )
         return got[:3], got[3:]
 
-    def attend_backward(self, segs, qkv, grads, turned, lse, hosted_steps):
+    def attend_backward(self, segs, order, qkv, grads, turned, lse, heads, hosted_steps):
         rows, wide = qkv.shape
-        plan, ins, outs, scratch, aliases = self.guests(hosted_steps, 6, 1)
+        plan, ins, outs, scratch, aliases = self.guests(hosted_steps, 7, 1)
         low = jnp.bfloat16
         got = self.call(
-            functools.partial(attend_backward_kernel, self.nf, self.nc, plan),
+            functools.partial(attend_backward_kernel, self.nf, self.nc, heads, plan),
             "attend_backward",
             (jax.ShapeDtypeStruct((rows, wide), low),) + tuple(outs),
-            [segs.reshape(1, rows), segs.reshape(rows, 1), qkv, grads, turned, lse] + ins,
-            [in_vmem()] * 6 + self.specs(hosted_steps),
+            [segs.reshape(1, rows), segs.reshape(rows, 1), qkv, grads, turned, lse, order] + ins,
+            [in_vmem()] * 6 + [in_smem()] + self.specs(hosted_steps),
             [in_vmem()] + [in_place()] * len(outs),
             [
                 pltpu.VMEM((rows, LANES), low),
@@ -2156,6 +2225,7 @@
     (attended, turned, lse), (expand, shrink, tangent) = net.attend_forward(
         segs,
         qkv,
+        heads_each,
         [
             (GatherStep, 2, [expand]),
             (GatherStep, 2, [shrink]),
@@ -2218,15 +2288,15 @@
     block_output = net.swap(out_rows.reshape(each, stretch_len, width), to_origin, to_column)
     attended_delta = jnp.dot(branch_delta, mixer, preferred_element_type=wide).astype(low)
     mixer_rows = outer_sum(branch_delta, attended).astype(low).reshape(nc, out_each, slots)
-    attended_delta = pick(attended_delta.reshape(nc, stretch_len, slots), inverse).reshape(
-        rows_all, slots
-    )
+    attended_delta = attended_delta.reshape(nc, stretch_len, slots)
     joint_delta, boxes = net.attend_backward(
         segs,
+        inverse,
         qkv,
         attended_delta,
         turned,
         lse,
+        heads_each,
         [(ScatterStep, 4, [expand_rows, *boxes[:2]]), (ScatterStep, 4, [shrink_rows, *boxes[2:]])],
     )
     expand_grad = net.total(expand_rows, *boxes[:2])
@@ -2235,25 +2305,16 @@
     normed_grad, (joint_grad, mixer_grad, expand_pieces, shrink_pieces) = (
         net.scatter_fsdp(
             "scatter_normed",
-            pick(joint_delta.reshape(nc, stretch_len, 3 * slots), positions).reshape(
-                rows_all, 3 * slots
-            ),
+            joint_delta,
             joint,
             True,
             [
                 (ScatterRing, nf * thin + rest, [joint_rows]),
                 (ScatterRing, 0, [mixer_rows]),
-                (
-                    TradeGuest,
-                    ("fsdp", None),
-                    [widen(expand_grad.reshape(unit_each, nf, depth).transpose(1, 0, 2))],
-                ),
-                (
-                    TradeGuest,
-                    ("fsdp", None),
-                    [widen(shrink_grad.T.reshape(nf, each * unit_each, out_each))],
-                ),
+                (WindowTrade, width, [widen(expand_grad)]),
+                (WindowTrade, nc * unit_each, [widen(shrink_grad)]),
             ],
+            positions,
         )
     )
     unit_own, inverse_own = normalize(own_tokens.astype(wide))
@@ -2315,9 +2376,13 @@
             joint_last.reshape(each * rest, columns),
         ]
     ).astype(wide)
-    expand_gradient = expand_pieces[..., :depth].reshape(nf * unit_each, depth).T.astype(wide)
-    shrink_pieces = shrink_pieces[..., :out_each].reshape(nf, each, unit_each, out_each)
-    shrink_pieces = shrink_pieces.transpose(1, 0, 2, 3)
+    at = shard * depth - window(shard, nf, width)[0]
+    expand_pieces = lax.dynamic_slice_in_dim(expand_pieces, at, depth, 2)
+    expand_gradient = expand_pieces.reshape(nf * unit_each, depth).T.astype(wide)
+    units = each * unit_each
+    at = shard * units - window(shard, nf, nf * units)[0]
+    shrink_pieces = lax.dynamic_slice_in_dim(shrink_pieces, at, units, 2)
+    shrink_pieces = shrink_pieces.reshape(nf, out_each, each, unit_each).transpose(2, 0, 3, 1)
     shrink_gradient = shrink_pieces.reshape(shrink_weight.shape).astype(wide)
 
     own_rows = lax.dynamic_index_in_dim(mixer_pieces, shard, 0, keepdims=False)[:, :span].T

time: 746 us -> 751 us (level)
  matrix products: 66.7 us -> 74.4 us
    convert_element_type x1 -> x3, local copies, waits for them, and re-layouts: 1.61 us -> 12.9 us  [the longest x1 5.86 us: local_fast(): expand_delta = (active_grad * slope).astype(low)]
    gather x8 -> x6, local copies, waits for them, and re-layouts: 17.8 us -> 10.5 us  [pick(): return blocks.at[order].get(mode='promise_in_bounds', unique_indices=True)]
where the time goes in v1:
time: 751 us; the launch traced here: 741 us
  Pallas kernels  520 us (69%)
  local copies, waits for them, and re-layouts  85.6 us (11%)
  matrix products  74.4 us (10%)
  other arithmetic  44.4 us (6%)
  starting transfers between devices  14.1 us (2%)
    pallas_call x12, Pallas kernels, call(): pl.pallas_call(kernel, out_shape=outs, in_specs=in_specs, out_specs=out_s...  520 us
    dot_general x4, matrix products, outer_sum(): lax.dot_general(left, right, (((0,), (0,)), ((), ())), preferred_element_...  32.3 us
  transfers between devices with their start and end apart: 4, of which 0 were waited for; matrix products, arithmetic and copies ran while one was open for 9% of the time, Pallas kernels for 9%

profile of v1, /device:TPU:0, one launch (start us, length us, event | category | flops | bytes accessed | tf_op | source)
XLA Modules:
  0.0 740.6 jit_solution(990653562333383347)
XLA Ops:
  9.4 3.8 reshape.621
  17.7 42.6 %shard_map.280 = (bf16[8,56,640]{2,1,0:T(8,128)(2,1)}, bf16[8,16,256]{2,1,0:T(8,128)(2,1)}, bf16[2,128,1600]{2,1,0:T(8,128)(2,1)}, bf16[2,16,128]{2,1,0:T(8,128)...) custom-call(bf16[8,56,640]{2,1,0:T(8,128)(2,1)} %fusion.30.refs_0_, ...), custom_call_target="tpu_custom_call" | custom-call | tf_op jit(solution)/shard_map/pallas_call | solution.py:1902
  66.9 1.7 reshape.626.refs_0_
  70.3 1.6 reshape.627.refs_2_
  71.9 102.2 %shard_map.281 = (bf16[1600,1536]{1,0:T(8,128)(2,1)}, bf16[8,200,512]{2,1,0:T(8,128)(2,1)}, bf16[8,200,1600]{2,1,0:T(8,128)(2,1)}, bf16[8,200,1600]{2,1,0:T(8,12...) custom-call(bf16[4,56,1536]{2,1,0:T(8,128)(2,1)} %reshape.626.refs_0_, ...), custom_call_target="tpu_custom_call" | custom-call | tf_op jit(solution)/shard_map/pallas_call | solution.py:1902
  175.0 4.9 collective-permute-start
  180.0 2.9 collective-permute-start.1
  190.6 3.1 gather_fusion.1
  197.3 2.2 fusion.3
  199.6 10.9 %add_convert_fusion.refs_2_ = bf16[1024,1536]{1,0:T(8,128)(2,1)} fusion(bf16[1024,1600]{1,0:T(8,128)(2,1)S(1)} %fusion.3, bf16[1600,1536]{1,0:T(8,128)(2,1)} %get-tuple-element.84.refs_1_, f32[1536]{0:T(1024)S(1)} %dynamic-slice_reduce_fusion.1), kind=kOutput, calls=%fused_computation.26 | convolution fusion | flops 5036310528 | bytes 11343872 | tf_op jit(solution)/shard_map/dot_general | solution.py:2223
  217.8 35.6 %shard_map.282 = (bf16[1024,512]{1,0:T(8,128)(2,1)}, f32[4,128,1024]{2,1,0:T(8,128)}, f32[4,2,1024]{2,1,0:T(2,128)}, bf16[8,200,1600]{2,1,0:T(8,128)(2,1)}, bf16...) custom-call(s32[1,1024]{1,0:T(1,128)} %bitcast.209, ...), custom_call_target="tpu_custom_call", output_to_operand_aliasing={{3}: (3, {}), {4}: (4, {})} | custom-call | tf_op jit(solution)/shard_map/pallas_call | solution.py:1902
  253.5 2.9 gather_fusion.3
  256.4 35.0 %shard_map.283 = (f32[256,1600]{1,0:T(8,128)}, bf16[8,200,1600]{2,1,0:T(8,128)(2,1)}, bf16[8,200,1600]{2,1,0:T(8,128)(2,1)}) custom-call(bf16[8,128,512]{2,1,0:T(8,128)(2,1)} %gather_fusion.3, bf16[1600,512]{1,0:T(8,128)(2,1)} %bitcast.193, bf16[8,200,1600]{2,1,0:T(8,128)(2,1)} %get-tuple-element.90.refs_2_, ...), custom_call_target="tpu_custom_call", output_to_operand_aliasing={{1}: (2, {}), {2}: (3, {})} | custom-call | tf_op jit(solution)/shard_map/pallas_call | solution.py:1902
  291.3 1.8 fusion.43
  294.8 24.1 %shard_map.284 = (bf16[4,256,1600]{2,1,0:T(8,128)(2,1)}, bf16[8,200,1600]{2,1,0:T(8,128)(2,1)}, bf16[8,200,1600]{2,1,0:T(8,128)(2,1)}) custom-call(bf16[256,1600]{1,0:T(8,128)(2,1)} %add_convert_fusion.2.refs_0_, bf16[8,200,1600]{2,1,0:T(8,128)(2,1)} %get-tuple-element.93.refs_1_, ...), custom_call_target="tpu_custom_call", output_to_operand_aliasing={{1}: (1, {}), {2}: (2, {})} | custom-call | tf_op jit(solution)/shard_map/pallas_call | solution.py:1902
  318.9 12.6 %multiply_convert_fusion = (bf16[1024,1600]{0,1:T(8,128)(2,1)}, f32[1024,1600]{0,1:T(8,128)}) fusion(f32[1600]{0:T(1024)S(1)} %add.332, bf16[1024,1600]{1,0:T(8,128)(2,1)} %bitcast.228, bf16[1600,1600]{1,0:T(8,128)(2,1)} %bitcast.174), kind=kOutput, calls=%fused_computation.24 | convolution fusion | flops 5259264000 | bytes 18233600 | tf_op jit(solution)/shard_map/dot_general | solution.py:46
  331.5 13.2 %convert_reduce_fusion = (bf16[1600]{0:T(1024)(128)(2,1)S(1)}, bf16[1024,1600]{0,1:T(8,128)(2,1)S(1)}) fusion(f32[1024,1600]{0,1:T(8,128)} %get-tuple-element.220, f32[1600]{0:T(1024)S(1)} %add.332, bf16[1024,1600]{1,0:T(8,128)(2,1)S(1)} %bitcast.227, bf16[1600,1600]{1,0:T(8,128)(2,1)S(1)} %bitcast.173), kind=kOutput, calls=%fused_computation.23 | convolution fusion | flops 5278923264 | bytes 18236800 | tf_op jit(solution)/shard_map/dot_general | solution.py:2261
  344.7 1.7 copy-done.11
  346.4 7.9 %convolution_convert_fusion.2 = bf16[1600,1600]{1,0:T(8,128)(2,1)} fusion(bf16[1024,1600]{0,1:T(8,128)(2,1)S(1)} %get-tuple-element.222, bf16[1024,1600]{1,0:T(8,128)(2,1)S(1)} %bitcast.229), kind=kOutput, calls=%fused_computation.9 | convolution fusion | flops 5245440000 | bytes 11673600 | tf_op jit(solution)/shard_map/dot_general | solution.py:52
  354.3 5.9 copy.96
  360.2 11.7 %convolution_convert_fusion.1 = bf16[1600,1600]{1,0:T(8,128)(2,1)} fusion(bf16[1024,1600]{1,0:T(8,128)(2,1)} %bitcast.226, bf16[1024,1600]{0,1:T(8,128)(2,1)} %get-tuple-element.219), kind=kOutput, calls=%fused_computation.8 | convolution fusion | flops 5245440000 | bytes 11673600 | tf_op jit(solution)/shard_map/dot_general | solution.py:52
  371.8 5.5 copy.95
  377.3 29.0 %shard_map.285 = (f32[256,1600]{1,0:T(8,128)}, bf16[200,1600]{1,0:T(8,128)(2,1)}, bf16[200,1600]{1,0:T(8,128)(2,1)}, bf16[200,1600]{1,0:T(8,128)(2,1)}, bf16[200,1600]{1,0:T(8,128)(2,1)}) custom-call(bf16[8,128,1600]{2,1,0:T(8,128)(2,1)} %bitcast.178, bf16[1600,1600]{1,0:T(8,128)(2,1)} %bitcast.175, bf16[8,200,1600]{2,1,0:T(8,128)(2,1)} %bitcast.162, ...), custom_call_target="tpu_custom_call" | custom-call | tf_op jit(solution)/shard_map/pallas_call | solution.py:1902
  406.4 2.3 multiply_reduce_fusion.1
  408.7 2.3 convert_reduce_fusion.4
  411.0 35.1 %shard_map.286 = (bf16[4,256,1600]{2,1,0:T(8,128)(2,1)}, bf16[200,1600]{1,0:T(8,128)(2,1)}, bf16[200,1600]{1,0:T(8,128)(2,1)}, bf16[200,1600]{1,0:T(8,128)(2,1)}, bf16[200,1600]{1,0:T(8,128)(2,1)}) custom-call(bf16[256,1600]{1,0:T(8,128)(2,1)} %get-tuple-element.197.refs_0_, bf16[8,200,1600]{2,1,0:T(8,128)(2,1)} %bitcast.163, ...), custom_call_target="tpu_custom_call" | custom-call | tf_op jit(solution)/shard_map/pallas_call | solution.py:1902
  446.2 5.5 convolution_convert_fusion.4
  451.6 38.7 %shard_map.287 = (f32[256,1600]{1,0:T(8,128)}, bf16[200,1600]{1,0:T(8,128)(2,1)}, bf16[200,1600]{1,0:T(8,128)(2,1)}, bf16[200,1600]{1,0:T(8,128)(2,1)}, bf16[200,1600]{1,0:T(8,128)(2,1)}) custom-call(bf16[8,128,1600]{2,1,0:T(8,128)(2,1)} %bitcast.177, bf16[1600,1600]{1,0:T(8,128)(2,1)} %bitcast.172, bf16[8,200,1600]{2,1,0:T(8,128)(2,1)} %bitcast.164, ...), custom_call_target="tpu_custom_call" | custom-call | tf_op jit(solution)/shard_map/pallas_call | solution.py:1902
  490.3 37.6 %shard_map.288 = (bf16[1024,1536]{1,0:T(8,128)(2,1)}, bf16[200,1600]{1,0:T(8,128)(2,1)}, bf16[200,1600]{1,0:T(8,128)(2,1)}, bf16[200,1600]{1,0:T(8,128)(2,1)}, bf16[200,1600]{1,0:T(8,128)(2,1)}) custom-call(s32[1,1024]{1,0:T(1,128)} %bitcast.210, s32[1024,1]{1,0:T(8,128)} %copy.93.refs_1_, bf16[1024,1536]{1,0:T(8,128)(2,1)} %add_convert_fusion.refs_2_, ...), custom_call_target="tpu_custom_call" | custom-call | tf_op jit(solution)/shard_map/pallas_call | solution.py:1902
  528.0 2.4 convert_reduce_fusion.1
  530.4 9.6 %convolution_convert_fusion.refs_3_ = bf16[1600,1536]{1,0:T(8,128)(2,1)} fusion(bf16[1024,1600]{1,0:T(8,128)(2,1)} %copy-done.10, bf16[1024,1536]{1,0:T(8,128)(2,1)} %get-tuple-element.116), kind=kOutput, calls=%fused_computation.7 | convolution fusion | flops 5035622400 | bytes 11337728 | tf_op jit(solution)/shard_map/dot_general | solution.py:52
  540.0 1.5 fusion.25
  542.4 2.0 fusion.27
  545.4 3.1 convolution_convert_fusion.3
  548.4 74.2 %shard_map.289 = (f32[256,1600]{1,0:T(8,128)}, bf16[200,1536]{1,0:T(8,128)(2,1)}, bf16[200,512]{1,0:T(8,128)(2,1)}, bf16[4,200,512]{2,1,0:T(8,128)(2,1)}, bf16[4,200,512]{2,1,0:T(8,128)(2,1)}) custom-call(bf16[8,128,1536]{2,1,0:T(8,128)(2,1)} %bitcast.179, bf16[1600,1536]{1,0:T(8,128)(2,1)} %get-tuple-element.84.refs_1_, s32[8]{0:T(128)} %copy-done.32, ...), custom_call_target="tpu_custom_call" | custom-call | tf_op jit(solution)/shard_map/pallas_call | solution.py:1902
  624.0 1.9 slice.130
  626.5 1.6 add_convert_fusion.1
  632.1 4.9 collective-permute-start.2
  639.3 2.9 dynamic-slice_convert_fusion
  643.6 1.6 fusion.21
  645.2 26.4 %shard_map.290 = (bf16[4,48,1536]{2,1,0:T(8,128)(2,1)}, bf16[4,8,1536]{2,1,0:T(8,128)(2,1)}, bf16[4,200,512]{2,1,0:T(8,128)(2,1)}, bf16[4,128,256]{2,1,0:T(8,128)(2,1)}, bf16[2,128,1600]{2,1,0:T(8,128)(2,1)}) custom-call(bf16[4,48,1536]{2,1,0:T(8,128)(2,1)} %bitcast.189, bf16[8,1536]{1,0:T(8,128)(2,1)} %slice.131.refs_1_, ...), custom_call_target="tpu_custom_call" | custom-call | tf_op jit(solution)/shard_map/pallas_call | solution.py:1902
  671.6 1.6 reduce_sum.214
  680.0 39.2 %shard_map.291 = (bf16[8,56,640]{2,1,0:T(8,128)(2,1)}, bf16[8,16,256]{2,1,0:T(8,128)(2,1)}) custom-call(bf16[8,56,640]{2,1,0:T(8,128)(2,1)} %pad.84.refs_0_, bf16[8,16,256]{2,1,0:T(8,128)(2,1)} %bitcast.205), custom_call_target="tpu_custom_call" | custom-call | tf_op jit(solution)/shard_map/pallas_call | solution.py:1902
  722.0 1.9 slice.139
  725.2 2.2 copy.104
  727.5 3.6 reshape.669
  731.1 1.6 copy.103
  738.5 1.7 gather_fusion.4
  (257 shorter events, 70.2 us)
Async XLA Ops:
  8.4 6.6 copy-start.15
  9.4 6.8 slice-start
  65.1 3.5 copy-start.18
  66.0 3.8 copy-start.17
  69.8 104.3 %copy-start.19 = (bf16[2,128,1600]{1,2,0:T(8,128)(2,1)S(1)}, bf16[2,128,1600]{1,2,0:T(8,128)(2,1)}, u32[]{:S(2)}) copy-start(bf16[2,128,1600]{1,2,0:T(8,128)(2,1)} %param.18) | copy-start | bytes 2457604
  70.3 113.1 %copy-start.46 = (s32[8]{0:T(128)S(1)}, s32[8]{0:T(128)}, u32[]{:S(2)}) copy-start(s32[8]{0:T(128)} %param.20) | copy-start | bytes 100
  70.3 115.6 %copy-start.1 = (bf16[2,128,1600]{2,1,0:T(8,128)(2,1)S(1)}, bf16[2,128,1600]{2,1,0:T(8,128)(2,1)}, u32[]{:S(2)}) copy-start(bf16[2,128,1600]{2,1,0:T(8,128)(2,1)} %get-tuple-element.74) | copy-start | bytes 2457604
  70.3 118.3 %copy-start.25 = (bf16[8,16,256]{2,1,0:T(8,128)(2,1)S(1)}, bf16[8,16,256]{2,1,0:T(8,128)(2,1)}, u32[]{:S(2)}) copy-start(bf16[8,16,256]{2,1,0:T(8,128)(2,1)} %get-tuple-element.83) | copy-start | bytes 196612
  175.0 39.1 %collective-permute-start = (bf16[128,1600]{0,1:T(8,128)(2,1)}, bf16[128,1600]{0,1:T(8,128)(2,1)}, u32[]{:S(2)}, u32[]{:S(2)}) collective-permute-start(bf16[128,1600]{0,1:T(8,128)(2,1)} %get-tuple-element.205), channel_id=1, source_target_pairs={{0,0},{1,8},{2,16},{3,24},{4,4},{5,12},{6,20},{7,28},{8,3},{9,11},... | collective-permute-start | bytes 1228808 | tf_op jit(solution)/shard_map/ppermute | solution.py:1925
  180.0 34.2 %collective-permute-start.1 = (bf16[128,1600]{0,1:T(8,128)(2,1)}, bf16[128,1600]{0,1:T(8,128)(2,1)}, u32[]{:S(2)}, u32[]{:S(2)}) collective-permute-start(bf16[128,1600]{0,1:T(8,128)(2,1)} %get-tuple-element.206), channel_id=1, source_target_pairs={{0,4},{1,12},{2,20},{3,28},{4,0},{5,8},{6,16},{7,24},{8,7},{9,15},... | collective-permute-start | bytes 1228808 | tf_op jit(solution)/shard_map/ppermute | solution.py:1925
  183.6 7.0 copy-start.32
  186.2 4.4 copy-start.33
  199.5 11.0 %copy-start.10 = (bf16[1024,1600]{1,0:T(8,128)(2,1)}, bf16[1024,1600]{1,0:T(8,128)(2,1)S(1)}, u32[]{:S(2)}) copy-start(bf16[1024,1600]{1,0:T(8,128)(2,1)S(1)} %fusion.3) | copy-start | bytes 9830404
  199.5 11.0 %copy-start.34 = (pred[4]{0:T(512)(128)(4,1)S(1)}, pred[4]{0:T(512)(128)(4,1)}, u32[]{:S(2)}) copy-start(pred[4]{0:T(512)(128)(4,1)} %iota_compare_fusion.6) | copy-start | bytes 16
  199.5 11.3 %copy-start.29 = (f32[8,200]{1,0:T(8,128)S(1)}, f32[8,200]{1,0:T(8,128)}, u32[]{:S(2)}) copy-start(f32[8,200]{1,0:T(8,128)} %get-tuple-element.186) | copy-start | bytes 19204
  199.6 11.4 %copy-start.28 = (f32[8,200]{1,0:T(8,128)S(1)}, f32[8,200]{1,0:T(8,128)}, u32[]{:S(2)}) copy-start(f32[8,200]{1,0:T(8,128)} %get-tuple-element.188) | copy-start | bytes 19204
  199.6 11.5 %copy-start.27 = (f32[8,200]{1,0:T(8,128)S(1)}, f32[8,200]{1,0:T(8,128)}, u32[]{:S(2)}) copy-start(f32[8,200]{1,0:T(8,128)} %get-tuple-element.187) | copy-start | bytes 19204
  199.6 11.6 %copy-start.26 = (f32[8,200]{1,0:T(8,128)S(1)}, f32[8,200]{1,0:T(8,128)}, u32[]{:S(2)}) copy-start(f32[8,200]{1,0:T(8,128)} %get-tuple-element.189) | copy-start | bytes 19204
  199.6 14.2 %copy-start.2 = (bf16[2,128,1600]{2,1,0:T(8,128)(2,1)S(1)}, bf16[2,128,1600]{2,1,0:T(8,128)(2,1)}, u32[]{:S(2)}) copy-start(bf16[2,128,1600]{2,1,0:T(8,128)(2,1)} %get-tuple-element.74) | copy-start | bytes 2457604
  199.6 14.2 %copy-start.31 = (f32[2,128]{1,0:T(2,128)S(1)}, f32[2,128]{1,0:T(2,128)}, u32[]{:S(2)}) copy-start(f32[2,128]{1,0:T(2,128)} %get-tuple-element.218) | copy-start | bytes 3076
  212.7 5.1 copy-start.24
  318.9 12.6 %copy-start = (bf16[8,200,1600]{2,1,0:T(8,128)(2,1)S(1)}, bf16[8,200,1600]{2,1,0:T(8,128)(2,1)}, u32[]{:S(2)}) copy-start(bf16[8,200,1600]{2,1,0:T(8,128)(2,1)} %get-tuple-element.97) | copy-start | bytes 15360004
  318.9 12.6 %copy-start.44 = (bf16[4,256,1600]{2,1,0:T(8,128)(2,1)S(1)}, bf16[4,256,1600]{2,1,0:T(8,128)(2,1)}, u32[]{:S(2)}) copy-start(bf16[4,256,1600]{2,1,0:T(8,128)(2,1)} %get-tuple-element.98) | copy-start | bytes 9830404
  331.5 14.9 %copy-start.45 = (bf16[4,256,1600]{2,1,0:T(8,128)(2,1)S(1)}, bf16[4,256,1600]{2,1,0:T(8,128)(2,1)}, u32[]{:S(2)}) copy-start(bf16[4,256,1600]{2,1,0:T(8,128)(2,1)} %get-tuple-element.95) | copy-start | bytes 9830404
  530.4 9.7 %copy-start.22 = (bf16[200,1600]{1,0:T(8,128)(2,1)S(1)}, bf16[200,1600]{1,0:T(8,128)(2,1)}, u32[]{:S(2)}) copy-start(bf16[200,1600]{1,0:T(8,128)(2,1)} %get-tuple-element.119) | copy-start | bytes 1920004
  530.4 9.7 %copy-start.23 = (bf16[200,1600]{1,0:T(8,128)(2,1)S(1)}, bf16[200,1600]{1,0:T(8,128)(2,1)}, u32[]{:S(2)}) copy-start(bf16[200,1600]{1,0:T(8,128)(2,1)} %get-tuple-element.120) | copy-start | bytes 1920004
  540.0 2.4 copy-start.21
  541.5 3.9 copy-start.9
  541.5 3.9 copy-start.43
  626.5 10.5 %copy-start.30 = (f32[256]{0:T(256)S(1)}, f32[256]{0:T(256)}, u32[]{:S(2)}) copy-start(f32[256]{0:T(256)} %get-tuple-element.217) | copy-start | bytes 3076
  628.2 8.8 %copy-start.4 = (f32[256,1600]{1,0:T(8,128)S(1)}, f32[256,1600]{1,0:T(8,128)}, u32[]{:S(2)}) copy-start(f32[256,1600]{1,0:T(8,128)} %get-tuple-element.123) | copy-start | bytes 4915204
  628.2 9.8 %copy-start.35 = (pred[8]{0:T(512)(128)(4,1)S(1)}, pred[8]{0:T(512)(128)(4,1)}, u32[]{:S(2)}) copy-start(pred[8]{0:T(512)(128)(4,1)} %get-tuple-element.239) | copy-start | bytes 28
  628.2 9.8 %copy-start.36 = (pred[8]{0:T(512)(128)(4,1)S(1)}, pred[8]{0:T(512)(128)(4,1)}, u32[]{:S(2)}) copy-start(pred[8]{0:T(512)(128)(4,1)} %get-tuple-element.240) | copy-start | bytes 28
  628.2 9.8 %copy-start.37 = (pred[8]{0:T(512)(128)(4,1)S(1)}, pred[8]{0:T(512)(128)(4,1)}, u32[]{:S(2)}) copy-start(pred[8]{0:T(512)(128)(4,1)} %get-tuple-element.237) | copy-start | bytes 28
  628.2 9.8 %copy-start.38 = (pred[8]{0:T(512)(128)(4,1)S(1)}, pred[8]{0:T(512)(128)(4,1)}, u32[]{:S(2)}) copy-start(pred[8]{0:T(512)(128)(4,1)} %get-tuple-element.238) | copy-start | bytes 28
  628.2 9.8 %copy-start.39 = (pred[8]{0:T(512)(128)(4,1)S(1)}, pred[8]{0:T(512)(128)(4,1)}, u32[]{:S(2)}) copy-start(pred[8]{0:T(512)(128)(4,1)} %get-tuple-element.235) | copy-start | bytes 28
  628.2 9.8 %copy-start.40 = (pred[8]{0:T(512)(128)(4,1)S(1)}, pred[8]{0:T(512)(128)(4,1)}, u32[]{:S(2)}) copy-start(pred[8]{0:T(512)(128)(4,1)} %get-tuple-element.236) | copy-start | bytes 28
  628.2 9.8 %copy-start.41 = (pred[8]{0:T(512)(128)(4,1)S(1)}, pred[8]{0:T(512)(128)(4,1)}, u32[]{:S(2)}) copy-start(pred[8]{0:T(512)(128)(4,1)} %get-tuple-element.233) | copy-start | bytes 28
  628.2 9.8 %copy-start.42 = (pred[8]{0:T(512)(128)(4,1)S(1)}, pred[8]{0:T(512)(128)(4,1)}, u32[]{:S(2)}) copy-start(pred[8]{0:T(512)(128)(4,1)} %get-tuple-element.234) | copy-start | bytes 28
  630.6 8.3 %copy-start.16 = (bf16[4,200,512]{2,1,0:T(8,128)(2,1)S(1)}, bf16[4,200,512]{2,1,0:T(8,128)(2,1)}, u32[]{:S(2)}) copy-start(bf16[4,200,512]{2,1,0:T(8,128)(2,1)} %get-tuple-element.131) | copy-start | bytes 2457604
  630.6 106.7 %collective-permute-start.3 = (bf16[128,1600]{0,1:T(8,128)(2,1)}, bf16[128,1600]{0,1:T(8,128)(2,1)}, u32[]{:S(2)}, u32[]{:S(2)}) collective-permute-start(bf16[128,1600]{0,1:T(8,128)(2,1)} %bitcast.203), channel_id=1, source_target_pairs={{0,4},{1,20},{2,28},{3,12},{4,0},{5,16},{6,24},{7,8},{8,5},{9,21},... | collective-permute-start | bytes 1228808 | tf_op jit(solution)/shard_map/ppermute | solution.py:1925
  632.1 105.2 %collective-permute-start.2 = (bf16[128,1600]{0,1:T(8,128)(2,1)}, bf16[128,1600]{0,1:T(8,128)(2,1)}, u32[]{:S(2)}, u32[]{:S(2)}) collective-permute-start(bf16[128,1600]{0,1:T(8,128)(2,1)} %bitcast.202), channel_id=1, source_target_pairs={{0,0},{1,16},{2,24},{3,8},{4,4},{5,20},{6,28},{7,12},{8,1},{9,17},... | collective-permute-start | bytes 1228808 | tf_op jit(solution)/shard_map/ppermute | solution.py:1925
  638.9 4.7 copy-start.5
  678.0 45.8 %copy-start.8 = (f32[4,200,400]{2,1,0:T(8,128)S(1)}, f32[4,200,400]{2,1,0:T(8,128)}, u32[]{:S(2)}) copy-start(f32[4,200,400]{2,1,0:T(8,128)} %dynamic-slice_convert_fusion) | copy-start | bytes 3840004
  725.2 5.8 copy-start.7
  727.5 5.2 copy-start.13
  727.5 6.8 copy-start.14
  731.1 4.6 copy-start.12
  (4 other events, 8.8 us)

commit v2 on v1

--- a/solution.py
+++ b/solution.py
@@ -1739,7 +1739,7 @@
         if ordered:
             rows = left_ref[operands[2][block * 2 + upper]]
         else:
-            rows = left_ref[block * 2 + upper]
+            rows = left_ref[pl.ds(pl.multiple_of(block * count + start, half), half), :]
         for at in range(0, width, 512):
             size = 512 if at + 1024 <= width else width - at
             if turned:
@@ -1993,8 +1993,9 @@
 
     def scatter_fsdp(self, name, left, right, turned, hosted_steps=(), order=None):
         count = left.shape[0] // self.nf
-        own = [left.reshape(2 * self.nf, count // 2, left.shape[1]), right]
-        own += [] if order is None else [order]
+        own = [left, right]
+        if order is not None:
+            own = [left.reshape(2 * self.nf, count // 2, left.shape[1]), right, order]
         plan, ins, outs, scratch, aliases = self.guests(hosted_steps, len(own), 1)
         block = (count, right.shape[0] if turned else right.shape[1])
         box = pltpu.VMEM(block, left.dtype)
@@ -2218,7 +2219,7 @@
     tokens = pick(tokens.reshape(nc, stretch_len, width), inverse)
     token_values = tokens.reshape(rows_all, width).astype(wide)
     unit_one, _ = normalize(token_values)
-    normed = (unit_one * gain_one + shift_one).astype(low)
+    normed = lax.optimization_barrier((unit_one * gain_one + shift_one).astype(low))
     qkv = (
         jnp.dot(normed, joint, preferred_element_type=wide) + joint_bias
     ).astype(low)
@@ -2299,8 +2300,8 @@
         heads_each,
         [(ScatterStep, 4, [expand_rows, *boxes[:2]]), (ScatterStep, 4, [shrink_rows, *boxes[2:]])],
     )
-    expand_grad = net.total(expand_rows, *boxes[:2])
-    shrink_grad = net.total(shrink_rows, *boxes[2:])
+    expand_grad = widen(net.total(expand_rows, *boxes[:2]))
+    shrink_grad = widen(net.total(shrink_rows, *boxes[2:]))
     joint_rows = outer_sum(normed, joint_delta).astype(low)
     normed_grad, (joint_grad, mixer_grad, expand_pieces, shrink_pieces) = (
         net.scatter_fsdp(
@@ -2311,8 +2312,8 @@
             [
                 (ScatterRing, nf * thin + rest, [joint_rows]),
                 (ScatterRing, 0, [mixer_rows]),
-                (WindowTrade, width, [widen(expand_grad)]),
-                (WindowTrade, nc * unit_each, [widen(shrink_grad)]),
+                (WindowTrade, width, [expand_grad]),
+                (WindowTrade, nc * unit_each, [shrink_grad]),
             ],
             positions,
         )

time: 751 us -> 729 us (0.971)
  local copies, waits for them, and re-layouts: 85.6 us -> 72.9 us
  matrix products: 74.4 us -> 66 us
    convert_element_type x2 -> x0, local copies, waits for them, and re-layouts: 11.3 us -> none  [the longest x1 5.86 us: local_fast(): expand_delta = (active_grad * slope).astype(low)]
where the time goes in v2:
time: 729 us; the launch traced here: 718 us
  Pallas kernels  520 us (71%)
  local copies, waits for them, and re-layouts  72.9 us (10%)
  matrix products  66 us (9%)
  other arithmetic  43 us (6%)
  starting transfers between devices  14.4 us (2%)
    pallas_call x12, Pallas kernels, call(): pl.pallas_call(kernel, out_shape=outs, in_specs=in_specs, out_specs=out_s...  520 us
    dot_general x4, matrix products, outer_sum(): lax.dot_general(left, right, (((0,), (0,)), ((), ())), preferred_element_...  30.2 us
  transfers between devices with their start and end apart: 4, of which 0 were waited for; matrix products, arithmetic and copies ran while one was open for 9% of the time, Pallas kernels for 9%

profile of v2, /device:TPU:0, one launch (start us, length us, event | category | flops | bytes accessed | tf_op | source)
XLA Modules:
  0.0 718.3 jit_solution(12481316882067026574)
XLA Ops:
  7.0 1.4 copy.80
  9.4 3.8 reshape.615
  17.7 42.6 %shard_map.280 = (bf16[8,56,640]{2,1,0:T(8,128)(2,1)}, bf16[8,16,256]{2,1,0:T(8,128)(2,1)}, bf16[2,128,1600]{2,1,0:T(8,128)(2,1)}, bf16[2,16,128]{2,1,0:T(8,128)...) custom-call(bf16[8,56,640]{2,1,0:T(8,128)(2,1)} %fusion.30.refs_0_, ...), custom_call_target="tpu_custom_call" | custom-call | tf_op jit(solution)/shard_map/pallas_call | solution.py:1902
  66.9 1.7 reshape.620.refs_0_
  70.3 1.6 reshape.621.refs_2_
  71.9 102.2 %shard_map.281 = (bf16[1600,1536]{1,0:T(8,128)(2,1)}, bf16[8,200,512]{2,1,0:T(8,128)(2,1)}, bf16[8,200,1600]{2,1,0:T(8,128)(2,1)}, bf16[8,200,1600]{2,1,0:T(8,12...) custom-call(bf16[4,56,1536]{2,1,0:T(8,128)(2,1)} %reshape.620.refs_0_, ...), custom_call_target="tpu_custom_call" | custom-call | tf_op jit(solution)/shard_map/pallas_call | solution.py:1902
  175.0 4.9 collective-permute-start
  179.9 3.2 collective-permute-start.1
  190.9 3.1 gather_fusion.1
  195.7 2.8 fusion.10
  199.3 10.1 %add_convert_fusion.refs_2_ = bf16[1024,1536]{1,0:T(8,128)(2,1)} fusion(bf16[1024,1600]{1,0:T(8,128)(2,1)} %fusion.10, bf16[1600,1536]{1,0:T(8,128)(2,1)} %get-tuple-element.84.refs_1_, f32[1536]{0:T(1024)S(1)} %dynamic-slice_reduce_fusion.1), kind=kOutput, calls=%fused_computation.26 | convolution fusion | flops 5036310528 | bytes 11343872 | tf_op jit(solution)/shard_map/dot_general | solution.py:2224
  216.7 35.6 %shard_map.282 = (bf16[1024,512]{1,0:T(8,128)(2,1)}, f32[4,128,1024]{2,1,0:T(8,128)}, f32[4,2,1024]{2,1,0:T(2,128)}, bf16[8,200,1600]{2,1,0:T(8,128)(2,1)}, bf16...) custom-call(s32[1,1024]{1,0:T(1,128)} %bitcast.206, ...), custom_call_target="tpu_custom_call", output_to_operand_aliasing={{3}: (3, {}), {4}: (4, {})} | custom-call | tf_op jit(solution)/shard_map/pallas_call | solution.py:1902
  252.3 2.9 gather_fusion.3
  255.3 35.0 %shard_map.283 = (f32[256,1600]{1,0:T(8,128)}, bf16[8,200,1600]{2,1,0:T(8,128)(2,1)}, bf16[8,200,1600]{2,1,0:T(8,128)(2,1)}) custom-call(bf16[1024,512]{1,0:T(8,128)(2,1)} %bitcast.178, bf16[1600,512]{1,0:T(8,128)(2,1)} %bitcast.190, bf16[8,200,1600]{2,1,0:T(8,128)(2,1)} %get-tuple-element.90.refs_2_, ...), custom_call_target="tpu_custom_call", output_to_operand_aliasing={{1}: (2, {}), {2}: (3, {})} | custom-call | tf_op jit(solution)/shard_map/pallas_call | solution.py:1902
  290.2 1.8 fusion.43
  293.6 24.1 %shard_map.284 = (bf16[4,256,1600]{2,1,0:T(8,128)(2,1)}, bf16[8,200,1600]{2,1,0:T(8,128)(2,1)}, bf16[8,200,1600]{2,1,0:T(8,128)(2,1)}) custom-call(bf16[256,1600]{1,0:T(8,128)(2,1)} %add_convert_fusion.2.refs_0_, bf16[8,200,1600]{2,1,0:T(8,128)(2,1)} %get-tuple-element.93.refs_1_, ...), custom_call_target="tpu_custom_call", output_to_operand_aliasing={{1}: (1, {}), {2}: (2, {})} | custom-call | tf_op jit(solution)/shard_map/pallas_call | solution.py:1902
  317.8 10.9 %multiply_convert_fusion = (bf16[1024,1600]{1,0:T(8,128)(2,1)S(1)}, f32[1024,1600]{1,0:T(8,128)S(1)}) fusion(f32[1600]{0:T(1024)S(1)} %add.332, bf16[1024,1600]{1,0:T(8,128)(2,1)} %bitcast.223, bf16[1600,1600]{1,0:T(8,128)(2,1)} %bitcast.172), kind=kOutput, calls=%fused_computation.23 | convolution fusion | flops 5259264000 | bytes 18233600 | tf_op jit(solution)/shard_map/dot_general | solution.py:46
  328.7 9.2 %convert_reduce_fusion = (bf16[1600]{0:T(1024)(128)(2,1)S(1)}, bf16[1024,1600]{1,0:T(8,128)(2,1)S(1)}) fusion(f32[1024,1600]{1,0:T(8,128)S(1)} %get-tuple-element.220, f32[1600]{0:T(1024)S(1)} %add.332, bf16[1024,1600]{1,0:T(8,128)(2,1)S(1)} %bitcast.221, bf16[1600,1600]{1,0:T(8,128)(2,1)S(1)} %bitcast.171), kind=kOutput, calls=%fused_computation.22 | convolution fusion | flops 5278923264 | bytes 18236800 | tf_op jit(solution)/shard_map/dot_general | solution.py:2262
  337.9 8.6 %convolution_convert_fusion.2 = bf16[1600,1600]{1,0:T(8,128)(2,1)} fusion(bf16[1024,1600]{1,0:T(8,128)(2,1)S(1)} %get-tuple-element.222.refs_0_, bf16[1024,1600]{1,0:T(8,128)(2,1)S(1)} %bitcast.224), kind=kOutput, calls=%fused_computation.9 | convolution fusion | flops 5245440000 | bytes 11673600 | tf_op jit(solution)/shard_map/dot_general | solution.py:52
  346.6 8.7 %convolution_convert_fusion.1 = bf16[1600,1600]{1,0:T(8,128)(2,1)} fusion(bf16[1024,1600]{1,0:T(8,128)(2,1)S(1)} %bitcast.222, bf16[1024,1600]{1,0:T(8,128)(2,1)S(1)} %get-tuple-element.219.refs_0_), kind=kOutput, calls=%fused_computation.8 | convolution fusion | flops 5245440000 | bytes 11673600 | tf_op jit(solution)/shard_map/dot_general | solution.py:52
  355.3 29.0 %shard_map.285 = (f32[256,1600]{1,0:T(8,128)}, bf16[200,1600]{1,0:T(8,128)(2,1)}, bf16[200,1600]{1,0:T(8,128)(2,1)}, bf16[200,1600]{1,0:T(8,128)(2,1)}, bf16[200,1600]{1,0:T(8,128)(2,1)}) custom-call(bf16[1024,1600]{1,0:T(8,128)(2,1)} %copy-done.11, bf16[1600,1600]{1,0:T(8,128)(2,1)} %bitcast.173, bf16[8,200,1600]{2,1,0:T(8,128)(2,1)} %bitcast.160, ...), custom_call_target="tpu_custom_call" | custom-call | tf_op jit(solution)/shard_map/pallas_call | solution.py:1902
  384.4 2.3 multiply_reduce_fusion.1
  386.7 2.3 convert_reduce_fusion.4
  389.0 35.1 %shard_map.286 = (bf16[4,256,1600]{2,1,0:T(8,128)(2,1)}, bf16[200,1600]{1,0:T(8,128)(2,1)}, bf16[200,1600]{1,0:T(8,128)(2,1)}, bf16[200,1600]{1,0:T(8,128)(2,1)}, bf16[200,1600]{1,0:T(8,128)(2,1)}) custom-call(bf16[256,1600]{1,0:T(8,128)(2,1)} %get-tuple-element.197.refs_0_, bf16[8,200,1600]{2,1,0:T(8,128)(2,1)} %bitcast.161, ...), custom_call_target="tpu_custom_call" | custom-call | tf_op jit(solution)/shard_map/pallas_call | solution.py:1902
  424.2 5.6 convolution_convert_fusion.4
  429.8 3.1 convolution_convert_fusion.3
  432.9 38.7 %shard_map.287 = (f32[256,1600]{1,0:T(8,128)}, bf16[200,1600]{1,0:T(8,128)(2,1)}, bf16[200,1600]{1,0:T(8,128)(2,1)}, bf16[200,1600]{1,0:T(8,128)(2,1)}, bf16[200,1600]{1,0:T(8,128)(2,1)}) custom-call(bf16[1024,1600]{1,0:T(8,128)(2,1)} %copy-done.10, bf16[1600,1600]{1,0:T(8,128)(2,1)} %bitcast.170, bf16[8,200,1600]{2,1,0:T(8,128)(2,1)} %bitcast.162, ...), custom_call_target="tpu_custom_call" | custom-call | tf_op jit(solution)/shard_map/pallas_call | solution.py:1902
  471.6 37.6 %shard_map.288 = (bf16[1024,1536]{1,0:T(8,128)(2,1)}, bf16[200,1600]{1,0:T(8,128)(2,1)}, bf16[200,1600]{1,0:T(8,128)(2,1)}, bf16[200,1600]{1,0:T(8,128)(2,1)}, bf16[200,1600]{1,0:T(8,128)(2,1)}) custom-call(s32[1,1024]{1,0:T(1,128)} %bitcast.207, s32[1024,1]{1,0:T(8,128)} %copy.93.refs_1_, bf16[1024,1536]{1,0:T(8,128)(2,1)} %add_convert_fusion.refs_2_, ...), custom_call_target="tpu_custom_call" | custom-call | tf_op jit(solution)/shard_map/pallas_call | solution.py:1902
  509.2 2.4 convert_reduce_fusion.1
  511.6 9.8 %convolution_convert_fusion.refs_3_ = bf16[1600,1536]{1,0:T(8,128)(2,1)} fusion(bf16[1024,1600]{1,0:T(8,128)(2,1)} %fusion.10, bf16[1024,1536]{1,0:T(8,128)(2,1)} %get-tuple-element.116), kind=kOutput, calls=%fused_computation.7 | convolution fusion | flops 5035622400 | bytes 11337728 | tf_op jit(solution)/shard_map/dot_general | solution.py:52
  521.4 1.5 fusion.25
  526.1 74.2 %shard_map.289 = (f32[256,1600]{1,0:T(8,128)}, bf16[200,1536]{1,0:T(8,128)(2,1)}, bf16[200,512]{1,0:T(8,128)(2,1)}, bf16[4,200,512]{2,1,0:T(8,128)(2,1)}, bf16[4,200,512]{2,1,0:T(8,128)(2,1)}) custom-call(bf16[8,128,1536]{2,1,0:T(8,128)(2,1)} %bitcast.175, bf16[1600,1536]{1,0:T(8,128)(2,1)} %get-tuple-element.84.refs_1_, s32[8]{0:T(128)} %copy-done.32, ...), custom_call_target="tpu_custom_call" | custom-call | tf_op jit(solution)/shard_map/pallas_call | solution.py:1902
  601.7 1.9 slice.130
  604.2 1.6 add_convert_fusion.1
  608.3 1.4 collective-permute-start.3
  609.7 4.9 collective-permute-start.2
  616.9 2.7 dynamic-slice_convert_fusion
  619.6 1.4 bitcast_convert_fusion
  621.1 1.6 fusion.21
  622.7 26.6 %shard_map.290 = (bf16[4,48,1536]{2,1,0:T(8,128)(2,1)}, bf16[4,8,1536]{2,1,0:T(8,128)(2,1)}, bf16[4,200,512]{2,1,0:T(8,128)(2,1)}, bf16[4,128,256]{2,1,0:T(8,128)(2,1)}, bf16[2,128,1600]{2,1,0:T(8,128)(2,1)}) custom-call(bf16[4,48,1536]{2,1,0:T(8,128)(2,1)} %bitcast.186, bf16[8,1536]{1,0:T(8,128)(2,1)} %slice.131.refs_1_, ...), custom_call_target="tpu_custom_call" | custom-call | tf_op jit(solution)/shard_map/pallas_call | solution.py:1902
  649.3 1.6 reduce_sum.214
  657.9 39.2 %shard_map.291 = (bf16[8,56,640]{2,1,0:T(8,128)(2,1)}, bf16[8,16,256]{2,1,0:T(8,128)(2,1)}) custom-call(bf16[8,56,640]{2,1,0:T(8,128)(2,1)} %pad.84.refs_0_, bf16[8,16,256]{2,1,0:T(8,128)(2,1)} %bitcast.202), custom_call_target="tpu_custom_call" | custom-call | tf_op jit(solution)/shard_map/pallas_call | solution.py:1902
  699.9 1.9 slice.139
  703.1 2.2 copy.104
  705.4 3.6 reshape.661
  709.0 1.6 copy.103
  712.2 1.4 copy.105
  716.4 1.7 gather_fusion.4
  (255 shorter events, 64.9 us)
Async XLA Ops:
  8.4 6.6 copy-start.15
  9.4 6.8 slice-start
  65.1 3.5 copy-start.18
  66.0 3.8 copy-start.17
  69.8 104.3 %copy-start.19 = (bf16[2,128,1600]{1,2,0:T(8,128)(2,1)S(1)}, bf16[2,128,1600]{1,2,0:T(8,128)(2,1)}, u32[]{:S(2)}) copy-start(bf16[2,128,1600]{1,2,0:T(8,128)(2,1)} %param.18) | copy-start | bytes 2457604
  70.3 113.4 %copy-start.46 = (s32[8]{0:T(128)S(1)}, s32[8]{0:T(128)}, u32[]{:S(2)}) copy-start(s32[8]{0:T(128)} %param.20) | copy-start | bytes 100
  70.3 115.9 %copy-start.1 = (bf16[2,128,1600]{2,1,0:T(8,128)(2,1)S(1)}, bf16[2,128,1600]{2,1,0:T(8,128)(2,1)}, u32[]{:S(2)}) copy-start(bf16[2,128,1600]{2,1,0:T(8,128)(2,1)} %get-tuple-element.74) | copy-start | bytes 2457604
  70.3 118.6 %copy-start.25 = (bf16[8,16,256]{2,1,0:T(8,128)(2,1)S(1)}, bf16[8,16,256]{2,1,0:T(8,128)(2,1)}, u32[]{:S(2)}) copy-start(bf16[8,16,256]{2,1,0:T(8,128)(2,1)} %get-tuple-element.83) | copy-start | bytes 196612
  175.0 38.0 %collective-permute-start = (bf16[128,1600]{0,1:T(8,128)(2,1)}, bf16[128,1600]{0,1:T(8,128)(2,1)}, u32[]{:S(2)}, u32[]{:S(2)}) collective-permute-start(bf16[128,1600]{0,1:T(8,128)(2,1)} %get-tuple-element.205), channel_id=1, source_target_pairs={{0,0},{1,8},{2,16},{3,24},{4,4},{5,12},{6,20},{7,28},{8,3},{9,11},... | collective-permute-start | bytes 1228808 | tf_op jit(solution)/shard_map/ppermute | solution.py:1925
  179.9 33.1 %collective-permute-start.1 = (bf16[128,1600]{0,1:T(8,128)(2,1)}, bf16[128,1600]{0,1:T(8,128)(2,1)}, u32[]{:S(2)}, u32[]{:S(2)}) collective-permute-start(bf16[128,1600]{0,1:T(8,128)(2,1)} %get-tuple-element.206), channel_id=1, source_target_pairs={{0,4},{1,12},{2,20},{3,28},{4,0},{5,8},{6,16},{7,24},{8,7},{9,15},... | collective-permute-start | bytes 1228808 | tf_op jit(solution)/shard_map/ppermute | solution.py:1925
  183.9 7.0 copy-start.32
  186.5 4.4 copy-start.33
  199.2 10.2 %copy-start.34 = (pred[4]{0:T(512)(128)(4,1)S(1)}, pred[4]{0:T(512)(128)(4,1)}, u32[]{:S(2)}) copy-start(pred[4]{0:T(512)(128)(4,1)} %iota_compare_fusion.6) | copy-start | bytes 16
  199.3 10.5 %copy-start.29 = (f32[8,200]{1,0:T(8,128)S(1)}, f32[8,200]{1,0:T(8,128)}, u32[]{:S(2)}) copy-start(f32[8,200]{1,0:T(8,128)} %get-tuple-element.186) | copy-start | bytes 19204
  199.3 10.6 %copy-start.28 = (f32[8,200]{1,0:T(8,128)S(1)}, f32[8,200]{1,0:T(8,128)}, u32[]{:S(2)}) copy-start(f32[8,200]{1,0:T(8,128)} %get-tuple-element.188) | copy-start | bytes 19204
  199.3 10.6 %copy-start.27 = (f32[8,200]{1,0:T(8,128)S(1)}, f32[8,200]{1,0:T(8,128)}, u32[]{:S(2)}) copy-start(f32[8,200]{1,0:T(8,128)} %get-tuple-element.187) | copy-start | bytes 19204
  199.3 10.7 %copy-start.26 = (f32[8,200]{1,0:T(8,128)S(1)}, f32[8,200]{1,0:T(8,128)}, u32[]{:S(2)}) copy-start(f32[8,200]{1,0:T(8,128)} %get-tuple-element.189) | copy-start | bytes 19204
  199.3 13.4 %copy-start.2 = (bf16[2,128,1600]{2,1,0:T(8,128)(2,1)S(1)}, bf16[2,128,1600]{2,1,0:T(8,128)(2,1)}, u32[]{:S(2)}) copy-start(bf16[2,128,1600]{2,1,0:T(8,128)(2,1)} %get-tuple-element.74) | copy-start | bytes 2457604
  199.3 13.3 %copy-start.31 = (f32[2,128]{1,0:T(2,128)S(1)}, f32[2,128]{1,0:T(2,128)}, u32[]{:S(2)}) copy-start(f32[2,128]{1,0:T(2,128)} %get-tuple-element.218) | copy-start | bytes 3076
  211.5 5.1 copy-start.24
  317.7 10.9 %copy-start = (bf16[8,200,1600]{2,1,0:T(8,128)(2,1)S(1)}, bf16[8,200,1600]{2,1,0:T(8,128)(2,1)}, u32[]{:S(2)}) copy-start(bf16[8,200,1600]{2,1,0:T(8,128)(2,1)} %get-tuple-element.97) | copy-start | bytes 15360004
  317.7 10.9 %copy-start.43 = (bf16[4,256,1600]{2,1,0:T(8,128)(2,1)S(1)}, bf16[4,256,1600]{2,1,0:T(8,128)(2,1)}, u32[]{:S(2)}) copy-start(bf16[4,256,1600]{2,1,0:T(8,128)(2,1)} %get-tuple-element.98) | copy-start | bytes 9830404
  328.6 17.9 %copy-start.10 = (bf16[1024,1600]{1,0:T(8,128)(2,1)}, bf16[1024,1600]{1,0:T(8,128)(2,1)S(1)}, u32[]{:S(2)}) copy-start(bf16[1024,1600]{1,0:T(8,128)(2,1)S(1)} %get-tuple-element.219.refs_0_) | copy-start | bytes 9830404
  328.7 9.2 %copy-start.44 = (bf16[4,256,1600]{2,1,0:T(8,128)(2,1)S(1)}, bf16[4,256,1600]{2,1,0:T(8,128)(2,1)}, u32[]{:S(2)}) copy-start(bf16[4,256,1600]{2,1,0:T(8,128)(2,1)} %get-tuple-element.95) | copy-start | bytes 9830404
  337.9 8.7 %copy-start.11 = (bf16[1024,1600]{1,0:T(8,128)(2,1)}, bf16[1024,1600]{1,0:T(8,128)(2,1)S(1)}, u32[]{:S(2)}) copy-start(bf16[1024,1600]{1,0:T(8,128)(2,1)S(1)} %get-tuple-element.222.refs_0_) | copy-start | bytes 9830404
  424.2 5.7 copy-start.9
  424.2 5.6 copy-start.45
  511.6 9.8 %copy-start.22 = (bf16[200,1600]{1,0:T(8,128)(2,1)S(1)}, bf16[200,1600]{1,0:T(8,128)(2,1)}, u32[]{:S(2)}) copy-start(bf16[200,1600]{1,0:T(8,128)(2,1)} %get-tuple-element.119) | copy-start | bytes 1920004
  511.6 9.8 %copy-start.23 = (bf16[200,1600]{1,0:T(8,128)(2,1)S(1)}, bf16[200,1600]{1,0:T(8,128)(2,1)}, u32[]{:S(2)}) copy-start(bf16[200,1600]{1,0:T(8,128)(2,1)} %get-tuple-element.120) | copy-start | bytes 1920004
  604.1 10.5 %copy-start.30 = (f32[256]{0:T(256)S(1)}, f32[256]{0:T(256)}, u32[]{:S(2)}) copy-start(f32[256]{0:T(256)} %get-tuple-element.217) | copy-start | bytes 3076
  605.8 8.8 %copy-start.4 = (f32[256,1600]{1,0:T(8,128)S(1)}, f32[256,1600]{1,0:T(8,128)}, u32[]{:S(2)}) copy-start(f32[256,1600]{1,0:T(8,128)} %get-tuple-element.123) | copy-start | bytes 4915204
  605.8 9.8 %copy-start.35 = (pred[8]{0:T(512)(128)(4,1)S(1)}, pred[8]{0:T(512)(128)(4,1)}, u32[]{:S(2)}) copy-start(pred[8]{0:T(512)(128)(4,1)} %get-tuple-element.239) | copy-start | bytes 28
  605.8 9.8 %copy-start.36 = (pred[8]{0:T(512)(128)(4,1)S(1)}, pred[8]{0:T(512)(128)(4,1)}, u32[]{:S(2)}) copy-start(pred[8]{0:T(512)(128)(4,1)} %get-tuple-element.240) | copy-start | bytes 28
  605.8 9.8 %copy-start.37 = (pred[8]{0:T(512)(128)(4,1)S(1)}, pred[8]{0:T(512)(128)(4,1)}, u32[]{:S(2)}) copy-start(pred[8]{0:T(512)(128)(4,1)} %get-tuple-element.237) | copy-start | bytes 28
  605.8 9.8 %copy-start.38 = (pred[8]{0:T(512)(128)(4,1)S(1)}, pred[8]{0:T(512)(128)(4,1)}, u32[]{:S(2)}) copy-start(pred[8]{0:T(512)(128)(4,1)} %get-tuple-element.238) | copy-start | bytes 28
  605.8 9.8 %copy-start.39 = (pred[8]{0:T(512)(128)(4,1)S(1)}, pred[8]{0:T(512)(128)(4,1)}, u32[]{:S(2)}) copy-start(pred[8]{0:T(512)(128)(4,1)} %get-tuple-element.235) | copy-start | bytes 28
  605.8 9.8 %copy-start.40 = (pred[8]{0:T(512)(128)(4,1)S(1)}, pred[8]{0:T(512)(128)(4,1)}, u32[]{:S(2)}) copy-start(pred[8]{0:T(512)(128)(4,1)} %get-tuple-element.236) | copy-start | bytes 28
  605.9 9.8 %copy-start.41 = (pred[8]{0:T(512)(128)(4,1)S(1)}, pred[8]{0:T(512)(128)(4,1)}, u32[]{:S(2)}) copy-start(pred[8]{0:T(512)(128)(4,1)} %get-tuple-element.233) | copy-start | bytes 28
  605.9 9.8 %copy-start.42 = (pred[8]{0:T(512)(128)(4,1)S(1)}, pred[8]{0:T(512)(128)(4,1)}, u32[]{:S(2)}) copy-start(pred[8]{0:T(512)(128)(4,1)} %get-tuple-element.234) | copy-start | bytes 28
  608.3 8.3 %copy-start.16 = (bf16[4,200,512]{2,1,0:T(8,128)(2,1)S(1)}, bf16[4,200,512]{2,1,0:T(8,128)(2,1)}, u32[]{:S(2)}) copy-start(bf16[4,200,512]{2,1,0:T(8,128)(2,1)} %get-tuple-element.131) | copy-start | bytes 2457604
  608.3 107.0 %collective-permute-start.3 = (bf16[128,1600]{0,1:T(8,128)(2,1)}, bf16[128,1600]{0,1:T(8,128)(2,1)}, u32[]{:S(2)}, u32[]{:S(2)}) collective-permute-start(bf16[128,1600]{0,1:T(8,128)(2,1)} %bitcast.200), channel_id=1, source_target_pairs={{0,4},{1,20},{2,28},{3,12},{4,0},{5,16},{6,24},{7,8},{8,5},{9,21},... | collective-permute-start | bytes 1228808 | tf_op jit(solution)/shard_map/ppermute | solution.py:1925
  609.7 105.5 %collective-permute-start.2 = (bf16[128,1600]{0,1:T(8,128)(2,1)}, bf16[128,1600]{0,1:T(8,128)(2,1)}, u32[]{:S(2)}, u32[]{:S(2)}) collective-permute-start(bf16[128,1600]{0,1:T(8,128)(2,1)} %bitcast.199), channel_id=1, source_target_pairs={{0,0},{1,16},{2,24},{3,8},{4,4},{5,20},{6,28},{7,12},{8,1},{9,17},... | collective-permute-start | bytes 1228808 | tf_op jit(solution)/shard_map/ppermute | solution.py:1925
  615.8 5.3 copy-start.5
  655.9 45.8 %copy-start.8 = (f32[4,200,400]{2,1,0:T(8,128)S(1)}, f32[4,200,400]{2,1,0:T(8,128)}, u32[]{:S(2)}) copy-start(f32[4,200,400]{2,1,0:T(8,128)} %dynamic-slice_convert_fusion) | copy-start | bytes 3840004
  703.1 5.9 copy-start.7
  705.4 5.2 copy-start.13
  705.4 6.8 copy-start.14
  709.0 4.6 copy-start.12
  (4 other events, 9.5 us)
